TPU v7x, 128 devices: a whole 4x4x4 slice. The times are simulated.
128 devices in a mesh: tp: 2 (over core), dp: 64 (over z, y, x).
Axes of the slice: x: 4, y: 4, z: 4, core: 2. Of those that a mesh axis runs over, the one named last changes fastest.
Arguments:
- hidden: bfloat16 [64, 1024, 576], P('dp')
- norm_w: bfloat16 [576], replicated
- embed: bfloat16 [49152, 576], P('tp')
- targets: int32 [64, 1024], P('dp')
- loss_mask: int32 [64, 1024], P('dp')
- token_ids: int32 [64, 1024], P('dp')
- grad_embed: bfloat16 [64, 1024, 576], P('dp')
Outputs:
- output 1: float32 [], replicated
- output 2: bfloat16 [64, 1024, 576], P('dp')
- output 3: float32 [576], replicated
- output 4: float32 [49152, 576], P('tp', 'dp')
All inputs are finite; a program needn't handle non-finite values.
Results may differ from a plain program's by a relative error of at most 0.001.
Values sent between devices are 32-bit elements.
A program may use at most 1 GiB of HBM per device.

v0:
```python
import jax
import jax.numpy as jnp
from jax import lax
from jax.sharding import PartitionSpec as P

RMS_EPS = 1e-6


def solution(mesh):
    def local_step(hidden, norm_w, embed, targets, loss_mask, token_ids, grad_embed):
        batch_local, seq_len, d_model = hidden.shape
        vocab_local = embed.shape[0]
        tokens = batch_local * seq_len
        vocab_start = lax.axis_index("tp") * vocab_local
        hidden32 = hidden.reshape(tokens, d_model).astype(jnp.float32)
        inv_rms = lax.rsqrt(jnp.mean(hidden32 * hidden32, axis=-1, keepdims=True) + RMS_EPS)
        unit_rows = hidden32 * inv_rms
        norm_gain = norm_w.astype(jnp.float32)
        z_rows = (unit_rows * norm_gain).astype(jnp.bfloat16)
        logits = jnp.einsum("td,vd->tv", z_rows, embed, preferred_element_type=jnp.float32)
        row_max = lax.pmax(jnp.max(logits, axis=-1, keepdims=True), "tp")
        shifted = jnp.exp(logits - row_max)
        sum_exp = lax.psum(jnp.sum(shifted, axis=-1, keepdims=True), "tp")
        is_target = jnp.arange(vocab_local)[None, :] == (targets.reshape(tokens, 1) - vocab_start)
        target_logit = lax.psum(jnp.sum(jnp.where(is_target, logits, 0.0), axis=-1, keepdims=True), "tp")
        log_norm = row_max + jnp.log(sum_exp)
        mask_rows = loss_mask.reshape(tokens, 1).astype(jnp.float32)
        token_count = lax.psum(jnp.sum(mask_rows), "dp")
        loss_val = lax.psum(jnp.sum(mask_rows * (log_norm - target_logit)), "dp") / token_count
        soft_probs = shifted / sum_exp
        dlogits = (jnp.where(is_target, soft_probs - 1.0, soft_probs) * (mask_rows / token_count)).astype(jnp.bfloat16)
        grad_z = lax.psum(jnp.dot(dlogits, embed, preferred_element_type=jnp.float32), "tp")
        head_grad = jnp.einsum("tv,td->vd", dlogits, z_rows, preferred_element_type=jnp.float32)
        head_grad = lax.psum_scatter(head_grad, "dp", scatter_dimension=1, tiled=True)
        local_ids = token_ids.reshape(tokens) - vocab_start
        local_ids = jnp.where((local_ids >= 0) & (local_ids < vocab_local), local_ids, vocab_local)
        lookup_grad = jax.ops.segment_sum(grad_embed.reshape(tokens, d_model).astype(jnp.float32), local_ids, num_segments=vocab_local)
        lookup_grad = lax.psum_scatter(lookup_grad, "dp", scatter_dimension=1, tiled=True)
        grad_gain = lax.psum(jnp.sum(grad_z * unit_rows, axis=0), "dp")
        grad_unit = grad_z * norm_gain
        grad_hidden = inv_rms * (grad_unit - unit_rows * jnp.mean(grad_unit * unit_rows, axis=-1, keepdims=True))
        return (loss_val, grad_hidden.astype(jnp.bfloat16).reshape(batch_local, seq_len, d_model), grad_gain, head_grad + lookup_grad)

    return jax.shard_map(local_step, mesh=mesh, in_specs=(P("dp"), P(), P("tp"), P("dp"), P("dp"), P("dp"), P("dp")), out_specs=(P(), P("dp"), P(), P("tp", "dp")), check_vma=False)
```

profile of v0, /device:TPU:1, one launch (start us, length us, event | category | flops | bytes accessed | tf_op | source)
XLA Modules:
  0.0 1141.6 jit_solution(5659158077837664777)
XLA Ops:
  7.2 0.0 all-reduce.6.cloned.1.call-start
  7.2 1.5 fusion.13
  8.8 0.7 convert_element_type.46
  9.5 0.0 copy-done.5
  9.5 0.6 copy-done.7
  10.1 1.6 fusion.17.clone.4
  11.6 0.0 copy-start.9
  11.6 0.0 copy-start.13
  11.7 52.4 %fusion.19 = (f32[1024]{0:T(1024)S(1)}, f32[1024,24576]{1,0:T(8,128)}) fusion(bf16[24576,576]{0,1:T(8,128)(2,1)} %param.9, bf16[1024,576]{0,1:T(8,128)(2,1)S(1)} %fusion.17.clone.4), kind=kOutput, calls=%fused_computation.34 | convolution fusion | flops 29016195072 | bytes 130158592 | tf_op jit(solution)/shard_map/td,vd->tv/dot_general | solution.py:20
  64.1 3.5 pmax.7
  67.6 0.0 copy-done.9
  67.6 0.6 convert_reduce_fusion
  68.2 153.2 %psum.45 = f32[]{:T(128)} all-reduce(f32[]{:T(128)} %convert_reduce_fusion), channel_id=1, replica_groups=mesh['tp'=2,'dp'=64] {'dp'}, use_global_device_ids=true, to_apply=%region_10.11 | all-reduce | flops 1 | bytes 8 | tf_op jit(solution)/shard_map/psum | solution.py:28
  221.3 0.7 convert_divide_fusion
  222.0 0.0 copy-done.13
  222.1 36.6 %fusion.2 = (f32[1024]{0:T(1024)S(1)}, f32[1024]{0:T(1024)S(1)}) fusion(f32[1024,24576]{1,0:T(8,128)} %get-tuple-element.13, f32[1024]{0:T(1024)S(1)} %bitcast.43, s32[1024]{0:T(1024)S(1)} %bitcast.45), kind=kLoop, calls=%fused_computation.7 | loop fusion | flops 125827072 | bytes 100679680 | tf_op jit(solution)/shard_map/reduce_sum | solution.py:23
  258.7 31.1 %all-reduce.2 = (f32[1024,1]{0,1:T(1,128)}, f32[1024,1]{0,1:T(1,128)S(1)}) all-reduce(f32[1024,1]{0,1:T(1,128)S(1)} %bitcast.52, f32[1024,1]{0,1:T(1,128)S(1)} %bitcast.51), channel_id=1, replica_groups=mesh['tp'=2,'dp'=64] {'tp'}, use_global_device_ids=true, to_apply=%region_6.7 | all-reduce | flops 2048 | bytes 16384 | tf_op jit(solution)/shard_map/psum | solution.py:25
  289.8 0.0 copy-done.3
  289.8 49.3 %fusion.1 = bf16[1024,24576]{1,0:T(8,128)(2,1)} fusion(f32[1024,24576]{1,0:T(8,128)} %get-tuple-element.13, f32[1024]{0:T(1024)S(1)} %bitcast.47, f32[1024]{0:T(1024)S(1)} %bitcast.48, s32[1024]{0:T(1024)S(1)} %bitcast.46, f32[1024]{0:T(1024)S(1)} %bitcast.44), kind=kLoop, calls=%fused_computation.3 | loop fusion | flops 176160768 | bytes 151011328 | tf_op jit(solution)/shard_map/convert_element_type | solution.py:31
  339.2 0.0 copy-done.11
  339.2 0.0 copy-start.14
  339.2 38.4 %fusion.20 = f32[1024,576]{0,1:T(8,128)} fusion(bf16[1024,24576]{1,0:T(8,128)(2,1)} %fusion.1, bf16[24576,576]{0,1:T(8,128)(2,1)} %param.9), kind=kOutput, calls=%fused_computation.35 | convolution fusion | flops 28991029248 | bytes 81002496 | tf_op jit(solution)/shard_map/dot_general | solution.py:32
  377.6 0.0 all-reduce.6.cloned.1.call-update
  377.6 0.3 all-reduce.8.cloned.1.call-start
  377.9 0.9 copy-done.2
  378.9 1.7 bitcast_convert_fusion
  380.6 2.1 copy.13
  382.7 20.1 %broadcast_in_dim.28 = f32[24576,576]{1,0:T(8,128)} broadcast(f32[]{:T(128)} %constant.9.clone.1), dimensions={} | broadcast | bytes 56623108 | tf_op jit(solution)/shard_map/broadcast_in_dim | solution.py:37
  402.7 128.3 %scatter_fusion = f32[24576,576]{1,0:T(8,128)} fusion(f32[24576,576]{1,0:T(8,128)} %broadcast_in_dim.28, s32[1024]{0:T(1024)S(1)} %bitcast.49, f32[1024,576]{1,0:T(8,128)S(1)} %copy.13), kind=kCustom, calls=%fused_computation | custom fusion | flops 589824 | bytes 7081984 | tf_op jit(solution)/shard_map/scatter-add | solution.py:37
  531.1 0.0 copy-start
  531.1 58.7 %copy.14 = f32[24576,576]{0,1:T(8,128)} copy(f32[24576,576]{1,0:T(8,128)} %scatter_fusion) | data formatting | bytes 113246208 | tf_op jit(solution)/shard_map/scatter-add | solution.py:37
  589.8 0.0 copy-done.6
  589.9 64.5 %convolution_add_fusion = f32[24576,576]{0,1:T(8,128)} fusion(f32[24576,576]{0,1:T(8,128)} %copy.14, bf16[1024,24576]{1,0:T(8,128)(2,1)} %fusion.1, bf16[1,1024,576]{1,2,0:T(8,128)(2,1)S(1)} %copy-done, f32[576]{0:T(1024)S(1)} %copy-done.8, f32[1024]{0:T(1024)S(1)} %copy-done.6), kind=kOutput, calls=%fused_computation.8 | convolution fusion | flops 29007544320 | bytes 164763904 | tf_op jit(solution)/shard_map/tv,td->vd/dot_general | solution.py:33
  654.4 0.0 copy-start.12
  654.4 0.0 copy-start.15
  654.4 0.0 all-reduce.8.cloned.1.call-update
  654.4 0.6 copy-done.16
  655.0 0.6 dynamic-slice
  656.3 0.0 copy-done.4
  656.3 0.0 copy-done.10
  656.3 0.0 copy-done.12
  656.3 0.0 copy-done.15
  656.3 0.6 fusion.18
  656.9 2.5 fusion.12
  659.4 153.4 %all-reduce.1 = (f32[]{:T(128)}, f32[576]{0:T(1024)}) all-reduce(f32[]{:T(128)} %fusion.18, f32[576]{0:T(1024)S(1)} %get-tuple-element.6), channel_id=1, replica_groups=mesh['tp'=2,'dp'=64] {'dp'}, use_global_device_ids=true, to_apply=%region_8.9 | all-reduce | flops 577 | bytes 4616 | tf_op jit(solution)/shard_map/psum | solution.py:29
  814.2 1.5 fusion.14
  815.7 315.0 %all-reduce.8.cloned.1.call-done = f32[24576,576]{0,1:T(8,128)} async-done(((f32[24576,576]{0,1:T(8,128)}), f32[24576,576]{0,1:T(8,128)}) %all-reduce.8.cloned.1.call-update) | async-done | bytes 56623120
  1130.7 2.9 constant_dynamic-slice_fusion
  (20 shorter events, 0.1 us)
Async XLA Ops:
  7.2 649.8 %all-reduce.6.cloned.1.call-start = ((), (), s32[]{:S(2)}) async-start(), calls=%async_computation | async-start | bytes 4718592 | tf_op jit(solution)/shard_map/psum | solution.py:32
  8.8 0.7 copy-start.5
  9.5 0.6 copy-start.7
  11.6 55.9 %copy-start.9 = (s32[1,1024]{1,0:T(1,128)S(1)}, s32[1,1024]{1,0:T(1,128)}, u32[]{:S(2)}) copy-start(s32[1,1024]{1,0:T(1,128)} %param.11) | copy-start | bytes 12292
  11.6 210.4 %copy-start.13 = (s32[1,1024]{1,0:T(1,128)S(1)}, s32[1,1024]{1,0:T(1,128)}, u32[]{:S(2)}) copy-start(s32[1,1024]{1,0:T(1,128)} %param.10) | copy-start | bytes 12292
  67.6 222.3 %copy-start.3 = (f32[1024,1]{0,1:T(1,128)}, f32[1024,1]{0,1:T(1,128)S(1)}, u32[]{:S(2)}) copy-start(f32[1024,1]{0,1:T(1,128)S(1)} %pmax.7) | copy-start | bytes 12292
  289.8 49.3 %copy-start.11 = (f32[1024,1]{0,1:T(1,128)}, f32[1024,1]{0,1:T(1,128)S(1)}, u32[]{:S(2)}) copy-start(f32[1024,1]{0,1:T(1,128)S(1)} %get-tuple-element.11) | copy-start | bytes 12292
  339.2 38.7 %copy-start.14 = (s32[1,1024]{1,0:T(1,128)S(1)}, s32[1,1024]{1,0:T(1,128)}, u32[]{:S(2)}) copy-start(s32[1,1024]{1,0:T(1,128)} %param.12) | copy-start | bytes 12292
  377.6 1.3 copy-start.2
  377.6 753.1 %all-reduce.8.cloned.1.call-start = ((), (), s32[]{:S(2)}) async-start(), calls=%async_computation.1 | async-start | bytes 113246208
  531.1 58.7 %copy-start = (bf16[1,1024,576]{1,2,0:T(8,128)(2,1)S(1)}, bf16[1,1024,576]{1,2,0:T(8,128)(2,1)}, u32[]{:S(2)}) copy-start(bf16[1,1024,576]{1,2,0:T(8,128)(2,1)} %param.7) | copy-start | bytes 3538948
  531.1 58.7 %copy-start.6 = (f32[1024]{0:T(1024)S(1)}, f32[1024]{0:T(1024)}, u32[]{:S(2)}) copy-start(f32[1024]{0:T(1024)} %copy-done.5) | copy-start | bytes 12292
  531.1 58.7 %copy-start.8 = (f32[576]{0:T(1024)S(1)}, f32[576]{0:T(1024)}, u32[]{:S(2)}) copy-start(f32[576]{0:T(1024)} %copy-done.7) | copy-start | bytes 6916
  654.4 0.7 copy-start.16
  654.4 1.9 copy-start.4
  654.4 1.9 copy-start.10
  654.4 1.9 copy-start.12
  654.4 1.9 copy-start.15
  656.9 157.2 %copy-start.1 = (f32[1024,576]{0,1:T(8,128)S(1)}, f32[1024,576]{0,1:T(8,128)}, u32[]{:S(2)}) copy-start(f32[1024,576]{0,1:T(8,128)} %all-reduce.6.cloned.1.call-done) | copy-start | bytes 7077892
Sparse Core Ops, SparseCore 0:
  377.7 19.9 all-reduce.5
  654.6 476.0 all-reduce.7
where the time goes:
time: 1150 us; the launch traced here: 1140 us
  blocking collectives  341 us (30%)
  waiting for transfers between devices  315 us (27%)
  other arithmetic  226 us (20%)
  matrix products  155 us (13%)
  local copies, waits for them, and re-layouts  86.6 us (8%)
  between operations  17.4 us (2%)
    unnamed x3, waiting for transfers between devices  315 us
    psum x1, blocking collectives, local_step(): lax.psum(jnp.sum(mask_rows * (log_norm - target_logit)), 'dp') / token_count  153 us
    psum x1, blocking collectives, local_step(): token_count = lax.psum(jnp.sum(mask_rows), 'dp')  153 us
    scatter-add x1, other arithmetic, local_step(): jax.ops.segment_sum(grad_embed.reshape(tokens, d_model).astype(jnp.float3...  128 us
    dot_general x1, matrix products, local_step(): jnp.einsum('tv,td->vd', dlogits, z_rows, preferred_element_type=jnp.float32)  64.5 us
    scatter-add x1, local copies, waits for them, and re-layouts, local_step(): jax.ops.segment_sum(grad_embed.reshape(tokens, d_model).astype(jnp.float3...  58.7 us
    dot_general x1, matrix products, local_step(): jnp.einsum('td,vd->tv', z_rows, embed, preferred_element_type=jnp.float32)  52.4 us
    convert_element_type x1, other arithmetic, local_step(): (jnp.where(is_target, soft_probs - 1.0, soft_probs) * (mask_rows / token_...  49.3 us
  transfers between devices with their start and end apart: 2, of which 1 were waited for; matrix products, arithmetic and copies ran while one was open for 25% of the time, Pallas kernels for 0%

commit v1 on v0

v1 whole, which is shorter than its diff:
```python
import functools

import jax
import jax.numpy as jnp
from jax import lax
from jax.experimental import pallas as pl
from jax.experimental.pallas import tpu as pltpu
from jax.sharding import Mesh, PartitionSpec as P

RMS_EPS = 1e-6
F32, BF16, I32 = jnp.float32, jnp.bfloat16, jnp.int32
D = 576
TOK = 1024
GX = 4
TT = GX * TOK
VL = 24576
VB = VL // GX
TS = 512
NS = TT // TS
V2 = 256
N2 = VB // V2
TB = 256
CH = 256
VMEM = pl.BlockSpec(memory_space=pltpu.VMEM)
ANY = pl.BlockSpec(memory_space=pl.ANY)


def prep_kernel(h_ref, ge_ref, w_ref, zf_ref, gf_ref):
    rows = h_ref[...].astype(F32)
    inv = lax.rsqrt(jnp.mean(rows * rows, axis=0, keepdims=True) + RMS_EPS)
    z = (rows * inv * w_ref[...].astype(F32)).astype(BF16)
    zf_ref[...] = z.astype(F32)
    gf_ref[...] = ge_ref[...].astype(F32)


def prep(h_t, ge_t, w):
    return pl.pallas_call(
        prep_kernel,
        out_shape=(jax.ShapeDtypeStruct((D, TOK), F32), jax.ShapeDtypeStruct((D, TOK), F32)),
        in_specs=[VMEM, VMEM, VMEM],
        out_specs=(VMEM, VMEM),
        compiler_params=pltpu.CompilerParams(vmem_limit_bytes=40 << 20),
    )(h_t, ge_t, w)


def forward_kernel(et_ref, zg_ref, tgt_ref, logit_ref, stat_ref, zb_ref, gb_ref, e_s, stage, ebuf, fbuf, esem, osem, fsem):
    vstart = lax.axis_index("x") * VB

    def ecopy(i, slot):
        cols = pl.ds(pl.multiple_of(vstart + i * 512, 128), 512)
        return pltpu.make_async_copy(et_ref.at[:, cols], ebuf.at[slot], esem.at[slot])

    def fcopy(i, slot):
        return pltpu.make_async_copy(zg_ref.at[i // 2, i % 2], fbuf.at[slot], fsem.at[slot])

    fcopy(0, 0).start()
    ecopy(0, 0).start()
    for i in range(2 * NS):
        if i + 1 < 2 * NS:
            fcopy(i + 1, (i + 1) % 2).start()
        fcopy(i, i % 2).wait()
        dst = zb_ref if i % 2 == 0 else gb_ref
        dst[i // 2] = fbuf[i % 2].astype(BF16)

    def ebody(i, _):
        slot = lax.rem(i, 2)

        @pl.when(i + 1 < VB // 512)
        def _():
            ecopy(i + 1, 1 - slot).start()

        ecopy(i, slot).wait()
        e_s[pl.ds(pl.multiple_of(i * 512, 512), 512), :] = ebuf[slot].T
        return 0

    lax.fori_loop(0, VB // 512, ebody, 0)
    iota = lax.broadcasted_iota(I32, (8, TB), 0)

    def ocopy(ts, half, slot):
        return pltpu.make_async_copy(stage.at[slot], logit_ref.at[ts, :, pl.ds(half * TB, TB)], osem.at[slot])

    def ts_body(ts, _):
        for half in range(2):
            @pl.when(ts > 0)
            def _():
                ocopy(ts, half, half).wait()

            lanes = slice(half * TB, half * TB + TB)
            zt = zb_ref[ts, :, lanes]
            tgt = tgt_ref[ts, 0:1, lanes] - vstart
            m8 = jnp.full((8, TB), -jnp.inf, F32)
            s8 = jnp.zeros((8, TB), F32)
            t8 = jnp.zeros((8, TB), F32)
            for vc in range(VB // CH):
                l = jnp.dot(e_s[vc * CH:(vc + 1) * CH, :], zt, preferred_element_type=F32)
                stage[half, vc * CH:(vc + 1) * CH, :] = l
                mn = m8
                for r in range(CH // 8):
                    mn = jnp.maximum(mn, l[r * 8:r * 8 + 8])
                s8 = s8 * jnp.exp(m8 - mn)
                m8 = mn
                for r in range(CH // 8):
                    lr = l[r * 8:r * 8 + 8]
                    s8 = s8 + jnp.exp(lr - mn)
                    t8 = t8 + jnp.where(iota == tgt - (vc * CH + r * 8), lr, 0.0)
            m = jnp.max(m8, axis=0, keepdims=True)
            stat_ref[ts, 0:1, lanes] = m
            stat_ref[ts, 1:2, lanes] = jnp.sum(s8 * jnp.exp(m8 - m), axis=0, keepdims=True)
            stat_ref[ts, 2:3, lanes] = jnp.sum(t8, axis=0, keepdims=True)
            ocopy(ts, half, half).start()
        return 0

    lax.fori_loop(0, NS, ts_body, 0)
    for half in range(2):
        ocopy(0, half, half).wait()


def forward(et, zg, tgt):
    return pl.pallas_call(
        forward_kernel,
        out_shape=(
            jax.ShapeDtypeStruct((NS, VB, TS), F32),
            jax.ShapeDtypeStruct((NS, 8, TS), F32),
            jax.ShapeDtypeStruct((NS, D, TS), BF16),
            jax.ShapeDtypeStruct((NS, D, TS), BF16),
        ),
        in_specs=[ANY, ANY, VMEM],
        out_specs=(ANY, VMEM, VMEM, VMEM),
        scratch_shapes=[
            pltpu.VMEM((VB, D), BF16),
            pltpu.VMEM((2, VB, TB), F32),
            pltpu.VMEM((2, D, 512), BF16),
            pltpu.VMEM((2, D, TS), F32),
            pltpu.SemaphoreType.DMA((2,)),
            pltpu.SemaphoreType.DMA((2,)),
            pltpu.SemaphoreType.DMA((2,)),
        ],
        compiler_params=pltpu.CompilerParams(vmem_limit_bytes=60 << 20),
    )(et, zg, tgt)


def backward_kernel(et_ref, zt_ref, gt_ref, row_ref, ids_ref, logit_ref, dz_ref, de_ref, lbuf, et_s, lsem, esem):
    vstart = lax.axis_index("x") * VB
    iota = lax.broadcasted_iota(I32, (V2, TS), 0)

    def lcopy(vc, slot):
        return pltpu.make_async_copy(logit_ref.at[:, pl.ds(vc * V2, V2), :], lbuf.at[slot], lsem.at[slot])

    def ecopy(vc, slot):
        cols = pl.ds(pl.multiple_of(vstart + vc * V2, 128), V2)
        return pltpu.make_async_copy(et_ref.at[:, cols], et_s.at[slot], esem.at[slot])

    for slot in range(2):
        lcopy(slot, slot).start()
        ecopy(slot, slot).start()
    dz_ref[...] = jnp.zeros_like(dz_ref)

    def v_body(vc, _):
        slot = lax.rem(vc, 2)
        lcopy(vc, slot).wait()
        ecopy(vc, slot).wait()
        et = et_s[slot]
        base = vstart + vc * V2
        acc = jnp.zeros((D, V2), F32)
        for ts in range(NS):
            p = jnp.exp(lbuf[slot, ts] - row_ref[ts, 0:1, :])
            d = (jnp.where(iota == ids_ref[ts, 0:1, :] - base, p - 1.0, p) * row_ref[ts, 1:2, :]).astype(BF16)
            dz_ref[ts] += jnp.dot(et, d, preferred_element_type=F32)
            acc += lax.dot_general(zt_ref[ts], d, (((1,), (1,)), ((), ())), preferred_element_type=F32)
            o = jnp.where(iota == ids_ref[ts, 1:2, :] - base, 1.0, 0.0).astype(BF16)
            acc += lax.dot_general(gt_ref[ts], o, (((1,), (1,)), ((), ())), preferred_element_type=F32)
        de_ref[vc] = acc
        nxt = jnp.minimum(vc + 2, N2 - 1)
        lcopy(nxt, slot).start()
        ecopy(nxt, slot).start()
        return 0

    lax.fori_loop(0, N2, v_body, 0)
    for slot in range(2):
        lcopy(0, slot).wait()
        ecopy(0, slot).wait()


def backward(et, zb, gb, row, ids, logit):
    return pl.pallas_call(
        backward_kernel,
        out_shape=(jax.ShapeDtypeStruct((NS, D, TS), F32), jax.ShapeDtypeStruct((N2, D, V2), F32)),
        in_specs=[ANY, VMEM, VMEM, VMEM, VMEM, ANY],
        out_specs=(VMEM, VMEM),
        scratch_shapes=[
            pltpu.VMEM((2, NS, V2, TS), F32),
            pltpu.VMEM((2, D, V2), BF16),
            pltpu.SemaphoreType.DMA((2,)),
            pltpu.SemaphoreType.DMA((2,)),
        ],
        compiler_params=pltpu.CompilerParams(vmem_limit_bytes=63 << 20),
    )(et, zb, gb, row, ids, logit)


def solution(mesh):
    mesh4 = Mesh(mesh.devices.reshape(2, 4, 4, 4), ("tp", "z", "y", "x"))

    def local_step(hidden, norm_w, embed, targets, loss_mask, token_ids, grad_embed):
        core, xi = lax.axis_index("tp"), lax.axis_index("x")
        h_t = hidden.reshape(TOK, D).T
        ge_t = grad_embed.reshape(TOK, D).T
        et = embed.T
        zf, gf = prep(h_t, ge_t, norm_w.reshape(D, 1))
        both = jnp.stack([zf, gf])
        half = lax.dynamic_slice(both, (0, 0, core * TS), (2, D, TS))
        zg = lax.all_gather(half, ("x", "tp"), axis=0)
        ints = jnp.stack([targets.reshape(TOK), token_ids.reshape(TOK), loss_mask.reshape(TOK)])
        ints_g = lax.all_gather(ints, "x", axis=0)
        ints_g = ints_g.reshape(GX, 3, 2, TS).transpose(0, 2, 1, 3).reshape(NS, 3, TS)
        ids = jnp.pad(ints_g[:, :2] - core * VL, ((0, 0), (0, 6), (0, 0)))
        logit, stat, zb, gb = forward(et, zg, ids)
        stats = lax.all_gather(stat[:, :3], ("tp", "x"), axis=0)
        m = jnp.max(stats[:, :, 0], axis=0)
        s = jnp.sum(stats[:, :, 1] * jnp.exp(stats[:, :, 0] - m), axis=0)
        lse = m + jnp.log(s)
        tgt_logit = jnp.sum(stats[:, :, 2], axis=0)
        mask_own = loss_mask.reshape(TOK).astype(F32)
        lse_own = lax.dynamic_slice(lse, (2 * xi, 0), (2, TS)).reshape(TOK)
        tgt_own = lax.dynamic_slice(tgt_logit, (2 * xi, 0), (2, TS)).reshape(TOK)
        sums = lax.psum(jnp.stack([jnp.sum(mask_own), jnp.sum(mask_own * (lse_own - tgt_own))]), ("tp", "z", "y", "x")) * 0.5
        count = sums[0]
        loss_val = sums[1] / count
        scale = ints_g[:, 2].astype(F32) / count
        row = jnp.pad(jnp.stack([lse, scale], axis=1), ((0, 0), (0, 6), (0, 0)))
        dz, de = backward(et, zb, gb, row, ids, logit)
        dz = lax.psum_scatter(dz.reshape(GX, 2, D, TS), "x", scatter_dimension=0, tiled=True)
        dz = lax.psum(dz, "tp").reshape(2, D, TS).transpose(1, 0, 2).reshape(D, TOK)
        de = de.transpose(1, 0, 2).reshape(D, 16, VB // 16).transpose(1, 0, 2)
        de = lax.psum_scatter(de, ("z", "y"), scatter_dimension=0, tiled=True)
        de = lax.all_to_all(de.reshape(64, 9, VB // 16), ("z", "y", "x"), 0, 0)
        de = de.reshape(16, GX, 9, VB // 16).transpose(2, 1, 0, 3).reshape(9, VL)
        rows = h_t.astype(F32)
        inv = lax.rsqrt(jnp.mean(rows * rows, axis=0, keepdims=True) + RMS_EPS)
        unit = rows * inv
        grad_gain = lax.psum(jnp.sum(dz * unit, axis=1), ("tp", "z", "y", "x")) * 0.5
        gu = dz * norm_w.astype(F32).reshape(D, 1)
        grad_hidden = inv * (gu - unit * jnp.mean(gu * unit, axis=0, keepdims=True))
        grad_hidden = grad_hidden.astype(BF16).T.reshape(1, TOK, D)
        return loss_val, grad_hidden, grad_gain, de.T

    dp = ("z", "y", "x")
    return jax.shard_map(
        local_step,
        mesh=mesh4,
        in_specs=(P(dp), P(), P("tp"), P(dp), P(dp), P(dp), P(dp)),
        out_specs=(P(), P(dp), P(), P("tp", dp)),
        check_vma=False,
    )
```

time: 1150 us -> 690 us (0.60)
  other arithmetic: 226 us -> 11.4 us
  Pallas kernels: 0 us -> 186 us
  blocking collectives: 341 us -> 164 us
  matrix products: 155 us -> 0 us
  waiting for transfers between devices: 315 us -> 235 us
  local copies, waits for them, and re-layouts: 86.6 us -> 66.5 us
    unnamed x3 -> x5, waiting for transfers between devices: 315 us -> 95.5 us
    psum x3 -> x2, blocking collectives: 338 us -> 132 us  [the longest x1 66.5 us: local_step(): lax.psum(jnp.sum(dz * unit, axis=1), ('tp', 'z', 'y', 'x')) * 0.5]
    pallas_call x0 -> x3, Pallas kernels: none -> 186 us  [the longest x1 112 us: backward(): pl.pallas_call(backward_kernel, out_shape=(jax.ShapeDtypeStruct((NS, D, T...]
    dot_general x3 -> x0, matrix products: 155 us -> none  [the longest x1 64.5 us: local_step(): jnp.einsum('tv,td->vd', dlogits, z_rows, preferred_element_type=jnp.float32)]
    scatter-add x1 -> x0, other arithmetic: 128 us -> none  [local_step(): jax.ops.segment_sum(grad_embed.reshape(tokens, d_model).astype(jnp.float3...]
    all_gather x0 -> x1, waiting for transfers between devices: none -> 85.6 us  [local_step(): zg = lax.all_gather(half, ('x', 'tp'), axis=0)]
    scatter-add x1 -> x0, local copies, waits for them, and re-layouts: 58.7 us -> none  [local_step(): jax.ops.segment_sum(grad_embed.reshape(tokens, d_model).astype(jnp.float3...]
    convert_element_type x3 -> x2, other arithmetic: 51.7 us -> 0.01 us  [the longest x1 0.01 us: local_step(): mask_own = loss_mask.reshape(TOK).astype(F32)]
  transfers between devices with their start and end apart: 2 -> 5, of which waited for: 1 -> 4; matrix products, arithmetic and copies ran while one was open for 25% -> 9% of each run, Pallas kernels for 0% -> 0%
where the time goes in v1:
time: 690 us; the launch traced here: 689 us
  waiting for transfers between devices  235 us (34%)
  Pallas kernels  186 us (27%)
  blocking collectives  164 us (24%)
  local copies, waits for them, and re-layouts  66.5 us (10%)
  between operations  16.4 us (2%)
  other arithmetic  11.4 us (2%)
  starting transfers between devices  8.81 us (1%)
    pallas_call x1, Pallas kernels, backward(): pl.pallas_call(backward_kernel, out_shape=(jax.ShapeDtypeStruct((NS, D, T...  112 us
    unnamed x5, waiting for transfers between devices  95.5 us
    all_gather x1, waiting for transfers between devices, local_step(): zg = lax.all_gather(half, ('x', 'tp'), axis=0)  85.6 us
    pallas_call x1, Pallas kernels, forward(): pl.pallas_call(forward_kernel, out_shape=(jax.ShapeDtypeStruct((NS, VB, T...  73.3 us
    psum x1, blocking collectives, local_step(): lax.psum(jnp.sum(dz * unit, axis=1), ('tp', 'z', 'y', 'x')) * 0.5  66.5 us
    psum x1, blocking collectives, local_step(): lax.psum(jnp.stack([jnp.sum(mask_own), jnp.sum(mask_own * (lse_own - tgt_...  65.4 us
    reduce_scatter x1, waiting for transfers between devices, local_step(): lax.psum_scatter(dz.reshape(GX, 2, D, TS), 'x', scatter_dimension=0, tile...  36 us
    transpose x2, local copies, waits for them, and re-layouts, local_step(): de = de.transpose(1, 0, 2).reshape(D, 16, VB // 16).transpose(1, 0, 2)  32.9 us
  transfers between devices with their start and end apart: 5, of which 4 were waited for; matrix products, arithmetic and copies ran while one was open for 9% of the time, Pallas kernels for 0%

profile of v1, /device:TPU:1, one launch (start us, length us, event | category | flops | bytes accessed | tf_op | source)
XLA Modules:
  0.0 688.6 jit_solution(11896267736447831617)
XLA Ops:
  7.2 0.0 all-gather.6.cloned.1.call-start
  7.2 0.8 reshape.100.w_ref
  8.1 1.3 copy-done
  9.3 1.3 copy-done.2
  10.6 0.6 shard_map.102
  11.2 1.7 fusion.9
  12.9 0.0 all-gather.6.cloned.1.call-update
  12.9 0.0 reduce-scatter.5.cloned.1.call-start
  13.0 0.6 copy-done.4
  13.7 10.2 %all-gather.3 = s32[4,3,1024]{2,1,0:T(4,128)S(1)} all-gather(s32[1,3,1024]{2,1,0:T(4,128)S(1)} %add_bitcast_fusion), channel_id=3, replica_groups=mesh['tp'=2,'z'=4,'y'=4,'x'=4] {'x'}, dimensions={0}, use_global_device_ids=true | all-gather | bytes 61440 | tf_op jit(solution)/shard_map/all_gather | solution.py:213
  23.9 0.7 pad.8.tgt_ref.ids_ref
  24.6 0.6 convert_reduce_fusion
  25.2 85.6 %all-gather.6.cloned.1.call-done = f32[16,576,512]{2,1,0:T(8,128)} async-done(((f32[2,576,512]{2,1,0:T(8,128)}), f32[16,576,512]{2,1,0:T(8,128)}) %all-gather.6.cloned.1.call-update) | async-done | bytes 18874384 | tf_op jit(solution)/shard_map/all_gather | solution.py:211
  110.7 73.3 %shard_map.103 = (f32[8,6144,512]{2,1,0:T(8,128)}, f32[8,8,512]{2,1,0:T(8,128)}, bf16[8,576,512]{2,1,0:T(8,128)(2,1)}, bf16[8,576,512]{2,1,0:T(8,128)(2,1)}) custom-call(bf16[576,24576]{1,0:T(8,128)(2,1)} %bitcast.64, f32[8,2,576,512]{3,2,1,0:T(8,128)} %bitcast.67, s32[8,8,512]{2,1,0:T(8,128)} %pad.8.tgt_ref.ids_ref), custom_call_target="tpu_custom_call" | custom-call | tf_op jit(solution)/shard_map/pallas_call | solution.py:119
  184.1 0.9 slice.34
  185.0 22.1 %all-gather.2 = f32[64,3,512]{2,0,1:T(8,128)S(1)} all-gather(f32[8,3,512]{2,0,1:T(8,128)S(1)} %copy.25), channel_id=4, replica_groups=mesh['tp'=2,'z'=4,'y'=4,'x'=4] {'tp','x'}, dimensions={0}, use_global_device_ids=true | all-gather | bytes 442368 | tf_op jit(solution)/shard_map/all_gather | solution.py:217
  207.2 0.6 multiply_reduce_fusion
  207.8 1.4 pad_maximum_fusion
  209.2 65.4 %psum.21 = f32[2]{0:T(128)S(1)} all-reduce(f32[2]{0:T(128)S(1)} %pad_maximum_fusion), channel_id=1, replica_groups=mesh['tp'=2,'z'=4,'y'=4,'x'=4] {'tp','z','y','x'}, use_global_device_ids=true, to_apply=%region_5.6 | all-reduce | flops 2 | bytes 16 | tf_op jit(solution)/shard_map/psum | solution.py:225
  274.6 0.6 fusion.16
  275.2 0.7 fusion.14
  275.9 0.7 select_maximum_fusion.row_ref
  276.6 112.2 %shard_map.104 = (f32[8,576,512]{2,1,0:T(8,128)}, f32[24,576,256]{2,1,0:T(8,128)}) custom-call(bf16[576,24576]{1,0:T(8,128)(2,1)} %bitcast.65, bf16[8,576,512]{2,1,0:T(8,128)(2,1)} %get-tuple-element.15.zt_ref, bf16[8,576,512]{2,1,0:T(8,128)(2,1)} %get-tuple-element.16.gt_ref, f32[8,8,512]{2,1,0:T(8,128)} %select_maximum_fusion.row_ref, ...), custom_call_target="tpu_custom_call" | custom-call | tf_op jit(solution)/shard_map/pallas_call | solution.py:185
  388.8 0.0 reduce-scatter.5.cloned.1.call-update
  388.8 0.3 reduce-scatter.7.cloned.1.call-start
  389.1 18.3 %copy.27 = f32[576,24,256]{2,1,0:T(8,128)} copy(f32[576,24,256]{2,0,1:T(8,128)} %bitcast.68) | data formatting | bytes 28311552 | tf_op jit(solution)/shard_map/transpose | solution.py:233
  407.3 16.3 %reshape.89 = f32[576,16,384]{2,1,0:T(8,128)} reshape(f32[576,24,256]{2,1,0:T(8,128)} %copy.27) | data formatting | bytes 28311552 | tf_op jit(solution)/shard_map/reshape | solution.py:233
  423.7 14.6 %copy.28 = f32[16,576,384]{2,1,0:T(8,128)} copy(f32[16,576,384]{2,0,1:T(8,128)} %bitcast.66) | data formatting | bytes 28311552 | tf_op jit(solution)/shard_map/transpose | solution.py:233
  438.3 0.0 reduce-scatter.7.cloned.1.call-update
  438.3 0.0 all-reduce.5.cloned.1.call-start
  438.4 36.0 %reduce-scatter.5.cloned.1.call-done = f32[1,2,576,512]{3,2,1,0:T(8,128)} async-done(((f32[4,2,576,512]{3,2,1,0:T(8,128)}), f32[1,2,576,512]{3,2,1,0:T(8,128)}) %reduce-scatter.5.cloned.1.call-update) | async-done | bytes 2359312 | tf_op jit(solution)/shard_map/reduce_scatter | solution.py:231
  474.4 3.4 copy.32
  477.8 0.0 all-reduce.5.cloned.1.call-update
  477.8 0.7 copy-done.5
  478.4 0.6 copy-done.1
  479.0 0.3 fusion.8
  480.7 95.4 %reduce-scatter.7.cloned.1.call-done = f32[1,576,384]{2,1,0:T(8,128)} async-done(((f32[16,576,384]{2,1,0:T(8,128)}), f32[1,576,384]{2,1,0:T(8,128)}) %reduce-scatter.7.cloned.1.call-update) | async-done | bytes 884752
  576.1 2.4 reshape.90
  578.4 8.4 %all-to-all-start = ((f32[64,9,384]{2,1,0:T(8,128)}), f32[64,9,384]{2,1,0:T(8,128)}, u32[]{:S(2)}, u32[]{:S(2)}) async-start(f32[64,9,384]{2,1,0:T(8,128)} %reshape.90), calls=%async_computation.1 | async-start | bytes 3145728 | tf_op jit(solution)/shard_map/all_to_all | solution.py:235
  586.9 18.2 %all-reduce.5.cloned.1.call-done = f32[576,1024]{1,0:T(8,128)} async-done(((f32[576,1024]{1,0:T(8,128)}), f32[576,1024]{1,0:T(8,128)}) %all-reduce.5.cloned.1.call-update) | async-done | bytes 2359312 | tf_op jit(solution)/shard_map/psum | solution.py:232
  605.1 2.5 fusion.7
  607.6 66.5 %psum.23 = f32[576]{0:T(1024)} all-reduce(f32[576]{0:T(1024)S(1)} %get-tuple-element.20), channel_id=1, replica_groups=mesh['tp'=2,'z'=4,'y'=4,'x'=4] {'tp','z','y','x'}, use_global_device_ids=true, to_apply=%region_11.12 | all-reduce | flops 576 | bytes 4608 | tf_op jit(solution)/shard_map/psum | solution.py:240
  674.1 1.3 broadcast_multiply_fusion
  675.4 1.5 fusion.10
  676.9 1.8 copy.36
  678.7 0.1 copy.30
  678.8 0.1 pad.23
  678.9 2.1 copy.34
  (29 shorter events, 0.3 us)
Async XLA Ops:
  7.2 103.6 %all-gather.6.cloned.1.call-start = ((), (), s32[]{:S(2)}) async-start(), calls=%async_computation.5 | async-start | bytes 21233664 | tf_op jit(solution)/shard_map/all_gather | solution.py:211
  8.0 1.3 copy-start
  9.3 1.3 copy-start.2
  12.9 0.7 copy-start.4
  12.9 0.7 copy-start.6
  12.9 0.7 copy-start.7
  12.9 461.5 %reduce-scatter.5.cloned.1.call-start = ((), (), s32[]{:S(2)}) async-start(), calls=%async_computation.3 | async-start | bytes 11796480 | tf_op jit(solution)/shard_map/reduce_scatter | solution.py:231
  388.8 187.3 %reduce-scatter.7.cloned.1.call-start = ((), (), s32[]{:S(2)}) async-start(), calls=%async_computation.6 | async-start | bytes 15040512
  438.3 166.8 %all-reduce.5.cloned.1.call-start = ((), (), s32[]{:S(2)}) async-start(), calls=%async_computation.4 | async-start | bytes 4718592 | tf_op jit(solution)/shard_map/psum | solution.py:232
  477.8 0.7 copy-start.5
  477.8 1.3 copy-start.1
  578.4 98.5 %all-to-all-start = ((f32[64,9,384]{2,1,0:T(8,128)}), f32[64,9,384]{2,1,0:T(8,128)}, u32[]{:S(2)}, u32[]{:S(2)}) async-start(f32[64,9,384]{2,1,0:T(8,128)} %reshape.90), calls=%async_computation.1 | async-start | bytes 3145728 | tf_op jit(solution)/shard_map/all_to_all | solution.py:235
  605.1 70.3 %copy-start.3 = (f32[576,1024]{1,0:T(8,128)S(1)}, f32[576,1024]{1,0:T(8,128)}, u32[]{:S(2)}) copy-start(f32[576,1024]{1,0:T(8,128)} %all-reduce.5.cloned.1.call-done) | copy-start | bytes 7077892
Sparse Core Ops, SparseCore 0:
  13.1 97.6 all-gather.5
  388.9 85.4 reduce-scatter.4
  477.9 98.0 reduce-scatter.6
  578.4 26.6 all-reduce.4

commit v2 on v1

v2 whole, which is shorter than its diff:
```python
import functools

import jax
import jax.numpy as jnp
from jax import lax
from jax.experimental import pallas as pl
from jax.experimental.pallas import tpu as pltpu
from jax.sharding import Mesh, PartitionSpec as P

RMS_EPS = 1e-6
F32, BF16, I32 = jnp.float32, jnp.bfloat16, jnp.int32
MESH = pl.DeviceIdType.MESH
D = 576
TOK = 1024
GX = 4
VL = 24576
VB = VL // GX
TS = 512
TB = 256
NS = GX * 2
V2 = 256
N2 = VB // V2
CH = 256
VMEM = pl.BlockSpec(memory_space=pltpu.VMEM)
ANY = pl.BlockSpec(memory_space=pl.ANY)
DELTA = (0, 3, 1, 2)
SLOT = {0: 0, 3: 1, 1: 2, 2: 3}


def remote(src, dst, send, recv, where):
    return pltpu.make_async_remote_copy(src_ref=src, dst_ref=dst, send_sem=send, recv_sem=recv, device_id=where, device_id_type=MESH)


def forward_kernel(
    h_ref, ge_ref, w_ref, ints_ref, et_ref,
    logit_ref, zb_out, uf_out, gf_out, row_ref, ids_ref, aux_ref,
    e_s, stage, ebuf, uf, zb, ints, stats, ny, nz,
    esem, osem, zsem, fsem, usend, urecv, psend, precv, isend, irecv, ssend, srecv, nsend, nrecv,
):
    core = lax.axis_index("tp")
    xi, yi, zi = lax.axis_index("x"), lax.axis_index("y"), lax.axis_index("z")
    other = 1 - core

    def at_x(d):
        return lax.rem(xi + d, 4)

    right, left = at_x(1), at_x(3)
    vstart = xi * VB

    def ecopy(i, slot):
        cols = pl.ds(pl.multiple_of(vstart + i * 512, 128), 512)
        return pltpu.make_async_copy(et_ref.at[:, cols], ebuf.at[slot], esem.at[slot])

    ecopy(0, 0).start()
    barrier = pltpu.get_barrier_semaphore()
    peers = [{"x": at_x(d)} for d in (1, 2, 3)] + [{"x": at_x(d), "tp": other} for d in range(4)]
    peers += [{"y": lax.rem(yi + d, 4)} for d in (1, 2, 3)] + [{"z": lax.rem(zi + d, 4)} for d in (1, 2, 3)]
    for peer in peers:
        pl.semaphore_signal(barrier, inc=1, device_id=peer, device_id_type=MESH)

    ints[0] = ints_ref[...]
    weight = w_ref[...].astype(F32)
    for half in range(2):
        for q in range(2):
            lo = half * TS + q * TB
            rows = h_ref[:, lo:lo + TB].astype(F32)
            inv = lax.rsqrt(jnp.mean(rows * rows, axis=0, keepdims=True) + RMS_EPS)
            uf[half, q] = rows * inv
    for q in range(2):
        lo = q * TB
        gf_out[q] = jnp.where(core == 0, ge_ref[:, lo:lo + TB].astype(F32), ge_ref[:, TS + lo:TS + lo + TB].astype(F32))
    pl.semaphore_wait(barrier, len(peers))

    def ucopy(src, q, dst, way, index):
        return remote(uf.at[2 * src + core, q], uf.at[2 * dst + core, q], usend.at[index], urecv.at[dst, q], {"x": way})

    def pcopy(r, q):
        return remote(uf.at[2 * r + core, q], uf.at[2 * r + core, q], psend.at[r, q], precv.at[r, q], {"tp": other})

    def parrive(r, q):
        return remote(uf.at[2 * r + core, q], uf.at[2 * r + other, q], psend.at[r, q], precv.at[r, q], {"tp": other})

    own = [ucopy(0, 0, 1, right, 0), ucopy(0, 0, 2, left, 1), ucopy(0, 1, 1, right, 2), ucopy(0, 1, 2, left, 3)]
    onward = [ucopy(1, 0, 3, right, 4), ucopy(2, 1, 3, left, 5)]

    def icopy(d):
        return remote(ints.at[0], ints.at[SLOT[(4 - d) % 4]], isend.at[d], irecv.at[SLOT[(4 - d) % 4]], {"x": at_x(d)})

    for copy in own[:2]:
        copy.start()
    for d in (1, 2, 3):
        icopy(d).start()
    for copy in own[2:]:
        copy.start()

    def ebody(i, _):
        slot = lax.rem(i, 2)

        @pl.when(i + 1 < VB // 512)
        def _():
            ecopy(i + 1, 1 - slot).start()

        ecopy(i, slot).wait()
        e_s[pl.ds(pl.multiple_of(i * 512, 512), 512), :] = ebuf[slot].T
        return 0

    lax.fori_loop(0, VB // 512, ebody, 0)

    def scopy(r, d, cross):
        index = 2 * d + cross
        where = {"x": at_x(d), "tp": other} if cross else {"x": at_x(d)}
        dst = SLOT[(DELTA[r] - d) % 4]
        return remote(stats.at[0, r], stats.at[index, dst], ssend.at[index, r], srecv.at[index, dst], where)

    def stat_copies(r):
        return [scopy(r, d, cross) for d in range(4) for cross in range(2) if d or cross]

    def ncopy(buf, axis, me, d):
        k = {"y": 0, "z": 1}[axis]
        return remote(buf.at[me], buf.at[me], nsend.at[k, d], nrecv.at[k, d], {axis: lax.rem(me + d, 4)})

    def narrive(buf, axis, me, d):
        k = {"y": 0, "z": 1}[axis]
        return remote(buf.at[me], buf.at[lax.rem(me + 4 - d, 4)], nsend.at[k, d], nrecv.at[k, d], {axis: lax.rem(me + d, 4)})

    iota = lax.broadcasted_iota(I32, (8, TB), 0)

    def ocopy(ts, q, slot):
        return pltpu.make_async_copy(stage.at[slot], logit_ref.at[ts, :, pl.ds(pl.multiple_of(q * TB, TB), TB)], osem.at[slot])

    def zcopy(ts, q):
        return pltpu.make_async_copy(zb.at[ts, q], zb_out.at[ts, q], zsem.at[ts, q])

    def fcopy(ts, q):
        return pltpu.make_async_copy(uf.at[ts, q], uf_out.at[ts, q], fsem.at[ts, q])

    def step(s, _):
        k, j = (s - 4) // 4, lax.rem(s, 4)
        r = jnp.where(s < 4, 0, jnp.where(s < 12, 1 + lax.rem(j, 2), 3))
        q = jnp.where(s < 4, lax.rem(j, 2), jnp.where(s < 12, k, lax.rem(j, 2)))
        half = jnp.where(s < 4, j // 2, jnp.where(j < 2, core, other))
        ts = 2 * r + half

        @pl.when(s == 4)
        def _():
            own[0].wait_recv()
            onward[0].start()
            pcopy(1, 0).start()
            own[1].wait_recv()
            pcopy(2, 0).start()
            for d in (1, 2, 3):
                icopy(d).wait_recv()
            for copy in stat_copies(0):
                copy.start()

        @pl.when(s == 6)
        def _():
            parrive(1, 0).wait_recv()
            parrive(2, 0).wait_recv()

        @pl.when(s == 8)
        def _():
            own[3].wait_recv()
            onward[1].start()
            pcopy(2, 1).start()
            own[2].wait_recv()
            pcopy(1, 1).start()
            count = jnp.sum(ints[:, :, :, 2, :].astype(F32))
            ny[yi] = jnp.full((8, 128), count, F32)
            for d in (1, 2, 3):
                ncopy(ny, "y", yi, d).start()

        @pl.when(s == 10)
        def _():
            parrive(1, 1).wait_recv()
            parrive(2, 1).wait_recv()
            for d in (1, 2, 3):
                narrive(ny, "y", yi, d).wait_recv()
            nz[zi] = ny[0] + ny[1] + ny[2] + ny[3]
            for d in (1, 2, 3):
                ncopy(nz, "z", zi, d).start()

        @pl.when(s == 12)
        def _():
            onward[0].wait_recv()
            pcopy(3, 0).start()
            onward[1].wait_recv()
            pcopy(3, 1).start()
            for copy in stat_copies(1) + stat_copies(2):
                copy.start()

        @pl.when(s == 14)
        def _():
            parrive(3, 0).wait_recv()
            parrive(3, 1).wait_recv()

        slot = lax.rem(s, 2)

        @pl.when(s >= 2)
        def _():
            ocopy(ts, q, slot).wait()

        zt = (uf[ts, q] * weight).astype(BF16)
        zb[ts, q] = zt
        zcopy(ts, q).start()
        fcopy(ts, q).start()
        tgt = ints[r, half, q, 0:1, :] - vstart
        m8 = jnp.full((8, TB), -jnp.inf, F32)
        s8 = jnp.zeros((8, TB), F32)
        t8 = jnp.zeros((8, TB), F32)
        for vc in range(VB // CH):
            l = jnp.dot(e_s[vc * CH:(vc + 1) * CH, :], zt, preferred_element_type=F32)
            stage[slot, vc * CH:(vc + 1) * CH, :] = l
            mn = m8
            for i in range(CH // 8):
                mn = jnp.maximum(mn, l[i * 8:i * 8 + 8])
            s8 = s8 * jnp.exp(m8 - mn)
            m8 = mn
            for i in range(CH // 8):
                li = l[i * 8:i * 8 + 8]
                s8 = s8 + jnp.exp(li - mn)
                t8 = t8 + jnp.where(iota == tgt - (vc * CH + i * 8), li, 0.0)
        m = jnp.max(m8, axis=0, keepdims=True)
        stats[0, r, half, q, 0:1, :] = m
        stats[0, r, half, q, 1:2, :] = jnp.sum(s8 * jnp.exp(m8 - m), axis=0, keepdims=True)
        stats[0, r, half, q, 2:3, :] = jnp.sum(t8, axis=0, keepdims=True)
        ocopy(ts, q, slot).start()
        return 0

    lax.fori_loop(0, 16, step, 0)
    for copy in stat_copies(3):
        copy.start()
    for d in (1, 2, 3):
        narrive(nz, "z", zi, d).wait_recv()
    total = (nz[0] + nz[1] + nz[2] + nz[3])[0:1, 0:1]
    for d in range(4):
        for cross in range(2):
            if d or cross:
                for r in range(4):
                    scopy(r, d, cross).wait_recv()
    loss = jnp.zeros((1, TB), F32)
    for r in range(4):
        for half in range(2):
            for q in range(2):
                lanes = slice(q * TB, q * TB + TB)
                ms = [stats[i, r, half, q, 0:1, :] for i in range(8)]
                m = functools.reduce(jnp.maximum, ms)
                tot = sum(stats[i, r, half, q, 1:2, :] * jnp.exp(ms[i] - m) for i in range(8))
                tgt_logit = sum(stats[i, r, half, q, 2:3, :] for i in range(8))
                lse = m + jnp.log(tot)
                mask = ints[r, half, q, 2:3, :].astype(F32)
                row_ref[2 * r + half, 0:1, lanes] = lse
                row_ref[2 * r + half, 1:2, lanes] = mask / total
                ids_ref[2 * r + half, 0:1, lanes] = ints[r, half, q, 0:1, :] - vstart
                ids_ref[2 * r + half, 1:2, lanes] = ints[r, half, q, 1:2, :] - vstart
                if r == 0:
                    loss = loss + jnp.where(core == half, mask * (lse - tgt_logit), 0.0)
    aux_ref[...] = jnp.zeros_like(aux_ref)
    aux_ref[0:1, :] = jnp.broadcast_to(jnp.sum(loss, axis=1, keepdims=True), (1, 128))
    aux_ref[1:2, :] = jnp.broadcast_to(total, (1, 128))
    for copy in own + onward:
        copy.wait_send()
    for r in (1, 2, 3):
        for q in range(2):
            pcopy(r, q).wait_send()
    for d in (1, 2, 3):
        icopy(d).wait_send()
        ncopy(ny, "y", yi, d).wait_send()
        ncopy(nz, "z", zi, d).wait_send()
    for r in range(4):
        for copy in stat_copies(r):
            copy.wait_send()
    for slot in range(2):
        ocopy(0, 0, slot).wait()
    for ts in range(NS):
        for q in range(2):
            zcopy(ts, q).wait()
            fcopy(ts, q).wait()


def forward(h_t, ge_t, w, ints, et):
    dma = pltpu.SemaphoreType.DMA
    return pl.pallas_call(
        forward_kernel,
        out_shape=(
            jax.ShapeDtypeStruct((NS, VB, TS), F32),
            jax.ShapeDtypeStruct((NS, 2, D, TB), BF16),
            jax.ShapeDtypeStruct((NS, 2, D, TB), F32),
            jax.ShapeDtypeStruct((2, D, TB), F32),
            jax.ShapeDtypeStruct((NS, 8, TS), F32),
            jax.ShapeDtypeStruct((NS, 8, TS), I32),
            jax.ShapeDtypeStruct((8, 128), F32),
        ),
        in_specs=[VMEM, VMEM, VMEM, VMEM, ANY],
        out_specs=(ANY, ANY, ANY, VMEM, VMEM, VMEM, VMEM),
        scratch_shapes=[
            pltpu.VMEM((VB, D), BF16),
            pltpu.VMEM((2, VB, TB), F32),
            pltpu.VMEM((2, D, 512), BF16),
            pltpu.VMEM((NS, 2, D, TB), F32),
            pltpu.VMEM((NS, 2, D, TB), BF16),
            pltpu.VMEM((4, 2, 2, 8, TB), I32),
            pltpu.VMEM((8, 4, 2, 2, 8, TB), F32),
            pltpu.VMEM((4, 8, 128), F32),
            pltpu.VMEM((4, 8, 128), F32),
            dma((2,)), dma((2,)), dma((NS, 2)), dma((NS, 2)), dma((6,)), dma((4, 2)), dma((4, 2)), dma((4, 2)),
            dma((4,)), dma((4,)), dma((8, 4)), dma((8, 4)), dma((2, 4)), dma((2, 4)),
        ],
        compiler_params=pltpu.CompilerParams(vmem_limit_bytes=62 << 20, collective_id=0, has_side_effects=True),
    )(h_t, ge_t, w, ints, et)


def backward_kernel(et_ref, zt_ref, gt_ref, row_ref, ids_ref, logit_ref, dz_ref, de_ref, lbuf, et_s, lsem, esem):
    vstart = lax.axis_index("x") * VB
    iota = lax.broadcasted_iota(I32, (V2, TS), 0)

    def lcopy(vc, slot):
        return pltpu.make_async_copy(logit_ref.at[:, pl.ds(vc * V2, V2), :], lbuf.at[slot], lsem.at[slot])

    def ecopy(vc, slot):
        cols = pl.ds(pl.multiple_of(vstart + vc * V2, 128), V2)
        return pltpu.make_async_copy(et_ref.at[:, cols], et_s.at[slot], esem.at[slot])

    for slot in range(2):
        lcopy(slot, slot).start()
        ecopy(slot, slot).start()
    dz_ref[...] = jnp.zeros_like(dz_ref)

    def v_body(vc, _):
        slot = lax.rem(vc, 2)
        lcopy(vc, slot).wait()
        ecopy(vc, slot).wait()
        et = et_s[slot]
        base = vstart + vc * V2
        acc = jnp.zeros((D, V2), F32)
        for ts in range(NS):
            p = jnp.exp(lbuf[slot, ts] - row_ref[ts, 0:1, :])
            d = (jnp.where(iota == ids_ref[ts, 0:1, :] - vc * V2, p - 1.0, p) * row_ref[ts, 1:2, :]).astype(BF16)
            dz_ref[ts] += jnp.dot(et, d, preferred_element_type=F32)
            acc += lax.dot_general(zt_ref[ts], d, (((1,), (1,)), ((), ())), preferred_element_type=F32)
            o = jnp.where(iota == ids_ref[ts, 1:2, :] - vc * V2, 1.0, 0.0).astype(BF16)
            acc += lax.dot_general(gt_ref[ts].astype(BF16), o, (((1,), (1,)), ((), ())), preferred_element_type=F32)
        de_ref[vc] = acc
        nxt = jnp.minimum(vc + 2, N2 - 1)
        lcopy(nxt, slot).start()
        ecopy(nxt, slot).start()
        return 0

    lax.fori_loop(0, N2, v_body, 0)
    for slot in range(2):
        lcopy(0, slot).wait()
        ecopy(0, slot).wait()


def backward(et, zb, gb, row, ids, logit):
    return pl.pallas_call(
        backward_kernel,
        out_shape=(jax.ShapeDtypeStruct((NS, D, TS), F32), jax.ShapeDtypeStruct((N2, D, V2), F32)),
        in_specs=[ANY, VMEM, VMEM, VMEM, VMEM, ANY],
        out_specs=(VMEM, VMEM),
        scratch_shapes=[
            pltpu.VMEM((2, NS, V2, TS), F32),
            pltpu.VMEM((2, D, V2), BF16),
            pltpu.SemaphoreType.DMA((2,)),
            pltpu.SemaphoreType.DMA((2,)),
        ],
        compiler_params=pltpu.CompilerParams(vmem_limit_bytes=63 << 20),
    )(et, zb, gb, row, ids, logit)


def solution(mesh):
    mesh4 = Mesh(mesh.devices.reshape(2, 4, 4, 4), ("tp", "z", "y", "x"))

    def local_step(hidden, norm_w, embed, targets, loss_mask, token_ids, grad_embed):
        core, xi = lax.axis_index("tp"), lax.axis_index("x")
        h_t = hidden.reshape(TOK, D).T
        ge_t = grad_embed.reshape(TOK, D).T
        et = embed.T
        own = [a.reshape(2, 2, 1, TB) for a in (targets - core * VL, token_ids - core * VL, loss_mask)]
        ints = jnp.pad(jnp.concatenate(own, axis=2), ((0, 0), (0, 0), (0, 5), (0, 0)))
        logit, zb, uf, gf, row, ids, aux = forward(h_t, ge_t, norm_w.reshape(D, 1), ints, et)
        gg = lax.all_gather(gf, ("x", "tp"), axis=0)
        order = jnp.array([0, 0, 3, 3, 1, 1, 2, 2])
        half = jnp.array([0, 1] * 4)
        rel = lax.rem(xi + order, 4) * 2 + half
        gb = jnp.take(gg.transpose(0, 2, 1, 3).reshape(8, D, TS), rel, axis=0)
        zc = zb.transpose(0, 2, 1, 3).reshape(8, D, TS)
        loss_val = lax.psum(aux[0, 0], ("tp", "z", "y", "x")) / aux[1, 0]
        dz, de = backward(et, zc, gb, row, ids, logit)
        back = lax.rem(jnp.array([0, 1, 2, 3]) + 4 - xi, 4)
        slot = jnp.take(jnp.array([0, 2, 3, 1]), back)
        dz = jnp.take(dz.reshape(GX, 2, D, TS), slot, axis=0)
        dz = lax.psum_scatter(dz, "x", scatter_dimension=0, tiled=True)
        dz = lax.psum(dz, "tp").reshape(2, D, TS).transpose(1, 0, 2).reshape(D, TOK)
        de = de.transpose(1, 0, 2).reshape(D, 16, VB // 16).transpose(1, 0, 2)
        de = lax.psum_scatter(de, ("z", "y"), scatter_dimension=0, tiled=True)
        de = lax.all_to_all(de.reshape(64, 9, VB // 16), ("z", "y", "x"), 0, 0)
        de = de.reshape(16, GX, 9, VB // 16).transpose(2, 1, 0, 3).reshape(9, VL)
        rows = h_t.astype(F32)
        inv = lax.rsqrt(jnp.mean(rows * rows, axis=0, keepdims=True) + RMS_EPS)
        unit = rows * inv
        grad_gain = lax.psum(jnp.sum(dz * unit, axis=1), ("tp", "z", "y", "x")) * 0.5
        gu = dz * norm_w.astype(F32).reshape(D, 1)
        grad_hidden = inv * (gu - unit * jnp.mean(gu * unit, axis=0, keepdims=True))
        grad_hidden = grad_hidden.astype(BF16).T.reshape(1, TOK, D)
        return loss_val, grad_hidden, grad_gain, de.T

    dp = ("z", "y", "x")
    return jax.shard_map(
        local_step,
        mesh=mesh4,
        in_specs=(P(dp), P(), P("tp"), P(dp), P(dp), P(dp), P(dp)),
        out_specs=(P(), P(dp), P(), P("tp", dp)),
        check_vma=False,
    )
```

time: 690 us -> 627 us (0.909)
  blocking collectives: 164 us -> 66.7 us
  local copies, waits for them, and re-layouts: 66.5 us -> 116 us
  waiting for transfers between devices: 235 us -> 201 us
  other arithmetic: 11.4 us -> 25.1 us
    psum x2 -> x1, blocking collectives: 132 us -> 66.7 us  [local_step(): loss_val = lax.psum(aux[0, 0], ('tp', 'z', 'y', 'x')) / aux[1, 0]]
    all_gather x1, waiting for transfers between devices: 85.6 us -> 47.9 us  [local_step(): gg = lax.all_gather(gf, ('x', 'tp'), axis=0)]
    all_gather x2 -> x0, blocking collectives: 32.3 us -> none  [the longest x1 22.1 us: local_step(): stats = lax.all_gather(stat[:, :3], ('tp', 'x'), axis=0)]
    reshape x2 -> x3, local copies, waits for them, and re-layouts: 0.84 us -> 19.3 us  [the longest x1 12.9 us: local_step(): gb = jnp.take(gg.transpose(0, 2, 1, 3).reshape(8, D, TS), rel, axis=0)]
    select_n x0 -> x3, other arithmetic: none -> 18.1 us  [the longest x1 9.08 us: local_step(): dz = jnp.take(dz.reshape(GX, 2, D, TS), slot, axis=0)]
    gather x0 -> x3, local copies, waits for them, and re-layouts: none -> 17.5 us  [the longest x1 8.49 us: local_step(): dz = jnp.take(dz.reshape(GX, 2, D, TS), slot, axis=0)]
    all_gather x0 -> x1, local copies, waits for them, and re-layouts: none -> 17 us  [local_step(): gg = lax.all_gather(gf, ('x', 'tp'), axis=0)]
  transfers between devices with their start and end apart: 5 -> 5, of which waited for: 4 -> 4; matrix products, arithmetic and copies ran while one was open for 9% -> 11% of each run, Pallas kernels for 0% -> 0%
where the time goes in v2:
time: 627 us; the launch traced here: 622 us
  waiting for transfers between devices  201 us (32%)
  Pallas kernels  188 us (30%)
  local copies, waits for them, and re-layouts  116 us (19%)
  blocking collectives  66.7 us (11%)
  other arithmetic  25.1 us (4%)
  between operations  16.8 us (3%)
  starting transfers between devices  8.96 us (1%)
    pallas_call x1, Pallas kernels, backward(): pl.pallas_call(backward_kernel, out_shape=(jax.ShapeDtypeStruct((NS, D, T...  114 us
    unnamed x5, waiting for transfers between devices  96.1 us
    pallas_call x1, Pallas kernels, forward(): pl.pallas_call(forward_kernel, out_shape=(jax.ShapeDtypeStruct((NS, VB, T...  73.7 us
    psum x1, blocking collectives, local_step(): loss_val = lax.psum(aux[0, 0], ('tp', 'z', 'y', 'x')) / aux[1, 0]  66.7 us
    all_gather x1, waiting for transfers between devices, local_step(): gg = lax.all_gather(gf, ('x', 'tp'), axis=0)  47.9 us
    reduce_scatter x1, waiting for transfers between devices, local_step(): dz = lax.psum_scatter(dz, 'x', scatter_dimension=0, tiled=True)  39 us
    transpose x2, local copies, waits for them, and re-layouts, local_step(): de = de.transpose(1, 0, 2).reshape(D, 16, VB // 16).transpose(1, 0, 2)  32.9 us
    psum x1, waiting for transfers between devices, local_step(): dz = lax.psum(dz, 'tp').reshape(2, D, TS).transpose(1, 0, 2).reshape(D, TOK)  18.2 us
  transfers between devices with their start and end apart: 5, of which 4 were waited for; matrix products, arithmetic and copies ran while one was open for 11% of the time, Pallas kernels for 0%

profile of v2, /device:TPU:1, one launch (start us, length us, event | category | flops | bytes accessed | tf_op | source)
XLA Modules:
  0.0 621.9 jit_solution(4879669078126885973)
XLA Ops:
  7.2 0.0 all-gather.3.cloned.1.call-start
  7.2 1.5 reshape.134.w_ref
  8.7 0.7 broadcast_subtract_fusion
  9.4 0.7 pad_add_fusion
  10.1 0.6 pad.4.ints_ref
  10.7 73.7 %shard_map.138 = (f32[8,6144,512]{2,1,0:T(8,128)}, bf16[8,2,576,256]{3,2,1,0:T(8,128)(2,1)}, f32[8,2,576,256]{3,2,1,0:T(8,128)}, f32[2,576,256]{2,1,0:T(8,128)},...) custom-call(bf16[576,1024]{1,0:T(8,128)(2,1)} %bitcast.51, bf16[576,1024]{1,0:T(8,128)(2,1)} %bitcast.62, ...), custom_call_target="tpu_custom_call" | custom-call | tf_op jit(solution)/shard_map/pallas_call | solution.py:283
  84.4 0.0 all-gather.3.cloned.1.call-update
  84.5 0.2 reduce-scatter.5.cloned.1.call-start
  84.7 0.0 copy-start
  84.7 0.0 copy-start.4
  84.7 0.0 copy-start.5
  84.7 4.9 copy.39
  89.6 0.6 gather_fusion
  90.3 47.9 %all-gather.3.cloned.1.call-done = f32[16,576,256]{2,1,0:T(8,128)} async-done(((f32[2,576,256]{2,1,0:T(8,128)}), f32[16,576,256]{2,1,0:T(8,128)}) %all-gather.3.cloned.1.call-update) | async-done | bytes 9437200 | tf_op jit(solution)/shard_map/all_gather | solution.py:382
  138.2 17.0 %copy.44 = f32[8,2,576,256]{3,1,2,0:T(2,128)} copy(f32[8,2,576,256]{3,2,1,0:T(8,128)} %bitcast.53) | data formatting | bytes 18874368 | tf_op jit(solution)/shard_map/all_gather | solution.py:382
  155.3 12.9 %reshape.96 = f32[8,576,512]{2,1,0:T(8,128)} reshape(f32[8,576,2,256]{3,2,1,0:T(2,128)} %bitcast.49) | data formatting | bytes 18874368 | tf_op jit(solution)/shard_map/reshape | solution.py:386
  168.2 8.4 %gather_fusion.1 = f32[8,576,512]{2,1,0:T(8,128)} fusion(f32[8,576,512]{2,1,0:T(8,128)} %reshape.96, s32[1024]{0:T(1024)S(1)} %pad_clamp_fusion.1), kind=kCustom, calls=%fused_computation.1 | custom fusion | bytes 18874400 | tf_op jit(solution)/shard_map/jit(_take)/gather | solution.py:386
  176.6 9.0 %broadcast_select_fusion.1.gt_ref = f32[8,576,512]{2,1,0:T(8,128)} fusion(f32[8,576,512]{2,1,0:T(8,128)} %gather_fusion.1, pred[8]{0:T(512)(128)(4,1)S(1)} %get-tuple-element.26), kind=kLoop, calls=%fused_computation.5 | loop fusion | flops 2359296 | bytes 18874376 | tf_op jit(solution)/shard_map/jit(_take)/select_n | solution.py:386
  185.5 113.8 %shard_map.139 = (f32[8,576,512]{2,1,0:T(8,128)}, f32[24,576,256]{2,1,0:T(8,128)}) custom-call(bf16[576,24576]{1,0:T(8,128)(2,1)} %bitcast.47, bf16[8,576,512]{2,1,0:T(8,128)(2,1)} %bitcast.50, f32[8,576,512]{2,1,0:T(8,128)} %broadcast_select_fusion.1.gt_ref, f32[8,8,512]{2,1,0:T(8,128)} %get-tuple-element.15.row_ref, ...), custom_call_target="tpu_custom_call" | custom-call | tf_op jit(solution)/shard_map/pallas_call | solution.py:356
  299.4 8.5 %gather_fusion.2 = f32[4,2,576,512]{3,2,1,0:T(8,128)} fusion(f32[4,2,576,512]{3,2,1,0:T(8,128)} %bitcast.55, s32[1024]{0:T(1024)S(1)} %pad_clamp_fusion), kind=kCustom, calls=%fused_computation.2 | custom fusion | bytes 18874384 | tf_op jit(solution)/shard_map/jit(_take)/gather | solution.py:392
  307.9 9.1 %broadcast_select_fusion = f32[4,2,576,512]{3,2,1,0:T(8,128)} fusion(f32[4,2,576,512]{3,2,1,0:T(8,128)} %gather_fusion.2, pred[4]{0:T(512)(128)(4,1)S(1)} %get-tuple-element.24), kind=kLoop, calls=%fused_computation.4 | loop fusion | flops 2359296 | bytes 18874372 | tf_op jit(solution)/shard_map/jit(_take)/select_n | solution.py:392
  316.9 0.0 reduce-scatter.5.cloned.1.call-update
  317.0 0.3 reduce-scatter.7.cloned.1.call-start
  317.2 18.3 %copy.34 = f32[576,24,256]{2,1,0:T(8,128)} copy(f32[576,24,256]{2,0,1:T(8,128)} %bitcast.52) | data formatting | bytes 28311552 | tf_op jit(solution)/shard_map/transpose | solution.py:395
  335.5 16.6 %reshape.101 = f32[576,16,384]{2,1,0:T(8,128)} reshape(f32[576,24,256]{2,1,0:T(8,128)} %copy.34) | data formatting | bytes 28311552 | tf_op jit(solution)/shard_map/reshape | solution.py:395
  352.1 14.6 %copy.35 = f32[16,576,384]{2,1,0:T(8,128)} copy(f32[16,576,384]{2,0,1:T(8,128)} %bitcast.48) | data formatting | bytes 28311552 | tf_op jit(solution)/shard_map/transpose | solution.py:395
  366.7 0.0 reduce-scatter.7.cloned.1.call-update
  366.7 0.0 all-reduce.5.cloned.1.call-start
  366.8 39.0 %reduce-scatter.5.cloned.1.call-done = f32[1,2,576,512]{3,2,1,0:T(8,128)} async-done(((f32[4,2,576,512]{3,2,1,0:T(8,128)}), f32[1,2,576,512]{3,2,1,0:T(8,128)}) %reduce-scatter.5.cloned.1.call-update) | async-done | bytes 2359312 | tf_op jit(solution)/shard_map/reduce_scatter | solution.py:393
  405.7 3.4 copy.40
  409.1 0.0 all-reduce.5.cloned.1.call-update
  409.1 0.7 copy-done.3
  409.8 1.3 fusion.14
  411.0 0.0 copy-done.1
  411.0 0.3 fusion.8
  411.3 96.0 %reduce-scatter.7.cloned.1.call-done = f32[1,576,384]{2,1,0:T(8,128)} async-done(((f32[16,576,384]{2,1,0:T(8,128)}), f32[1,576,384]{2,1,0:T(8,128)}) %reduce-scatter.7.cloned.1.call-update) | async-done | bytes 884752
  507.3 2.4 reshape.102
  509.7 8.4 %all-to-all-start = ((f32[64,9,384]{2,1,0:T(8,128)}), f32[64,9,384]{2,1,0:T(8,128)}, u32[]{:S(2)}, u32[]{:S(2)}) async-start(f32[64,9,384]{2,1,0:T(8,128)} %reshape.102), calls=%async_computation.1 | async-start | bytes 3145728 | tf_op jit(solution)/shard_map/all_to_all | solution.py:397
  518.1 18.2 %all-reduce.5.cloned.1.call-done = f32[576,1024]{1,0:T(8,128)} async-done(((f32[576,1024]{1,0:T(8,128)}), f32[576,1024]{1,0:T(8,128)}) %all-reduce.5.cloned.1.call-update) | async-done | bytes 2359312 | tf_op jit(solution)/shard_map/psum | solution.py:394
  536.4 2.5 fusion.7
  538.9 66.7 %all-reduce.2 = (f32[]{:T(128)}, f32[576]{0:T(1024)}) all-reduce(f32[]{:T(128)} %bitcast.8, f32[576]{0:T(1024)S(1)} %get-tuple-element.20), channel_id=1, replica_groups=mesh['tp'=2,'z'=4,'y'=4,'x'=4] {'tp','z','y','x'}, use_global_device_ids=true, to_apply=%region_0.1 | all-reduce | flops 577 | bytes 4616 | tf_op jit(solution)/shard_map/psum | solution.py:388
  606.9 1.3 broadcast_multiply_fusion
  608.2 1.5 fusion.9
  609.7 0.0 all-to-all-done
  609.8 1.8 copy.45
  611.5 0.1 copy.37
  611.6 0.1 pad.11
  611.7 2.1 copy.41
  (16 shorter events, 0.1 us)
Async XLA Ops:
  7.2 131.1 %all-gather.3.cloned.1.call-start = ((), (), s32[]{:S(2)}) async-start(), calls=%async_computation.5 | async-start | bytes 10616832 | tf_op jit(solution)/shard_map/all_gather | solution.py:382
  84.5 321.2 %reduce-scatter.5.cloned.1.call-start = ((), (), s32[]{:S(2)}) async-start(), calls=%async_computation.3 | async-start | bytes 11796480 | tf_op jit(solution)/shard_map/reduce_scatter | solution.py:393
  84.7 4.9 copy-start
  84.7 5.5 copy-start.4
  84.7 5.5 copy-start.5
  317.0 190.4 %reduce-scatter.7.cloned.1.call-start = ((), (), s32[]{:S(2)}) async-start(), calls=%async_computation.6 | async-start | bytes 15040512
  366.7 169.7 %all-reduce.5.cloned.1.call-start = ((), (), s32[]{:S(2)}) async-start(), calls=%async_computation.4 | async-start | bytes 4718592 | tf_op jit(solution)/shard_map/psum | solution.py:394
  409.1 0.7 copy-start.3
  409.1 2.0 copy-start.1
  509.7 100.0 %all-to-all-start = ((f32[64,9,384]{2,1,0:T(8,128)}), f32[64,9,384]{2,1,0:T(8,128)}, u32[]{:S(2)}, u32[]{:S(2)}) async-start(f32[64,9,384]{2,1,0:T(8,128)} %reshape.102), calls=%async_computation.1 | async-start | bytes 3145728 | tf_op jit(solution)/shard_map/all_to_all | solution.py:397
  536.4 71.8 %copy-start.2 = (f32[576,1024]{1,0:T(8,128)S(1)}, f32[576,1024]{1,0:T(8,128)}, u32[]{:S(2)}) copy-start(f32[576,1024]{1,0:T(8,128)} %all-reduce.5.cloned.1.call-done) | copy-start | bytes 7077892
Sparse Core Ops, SparseCore 0:
  84.6 53.6 all-gather.2
  317.1 88.5 reduce-scatter.4
  409.2 98.0 reduce-scatter.6
  509.6 26.6 all-reduce.4

commit v3 on v2

v3 whole, which is shorter than its diff:
```python
import functools

import jax
import jax.numpy as jnp
from jax import lax
from jax.experimental import pallas as pl
from jax.experimental.pallas import tpu as pltpu
from jax.sharding import Mesh, PartitionSpec as P

RMS_EPS = 1e-6
F32, BF16, I32 = jnp.float32, jnp.bfloat16, jnp.int32
MESH = pl.DeviceIdType.MESH
D = 576
TOK = 1024
GX = 4
VL = 24576
VB = VL // GX
TS = 512
TB = 256
NS = GX * 2
V2 = 256
N2 = VB // V2
CH = 256
ROWS, LANE, OWN = 144, 128, 9
HROWS, HD, EC = ROWS // 2, D // 2, 512
VMEM = pl.BlockSpec(memory_space=pltpu.VMEM)
ANY = pl.BlockSpec(memory_space=pl.ANY)
V, DMA, SDS = pltpu.VMEM, pltpu.SemaphoreType.DMA, jax.ShapeDtypeStruct
SUB = 8
TOKENS = (NS, 2, D, TB)
SUMS = (SUB, 640)
GRID = [(dy, dx) for dy in range(4) for dx in range(4)]
FAR = GRID[1:]
GROUP = [(d, cross) for d in range(4) for cross in range(2) if d or cross]
PAIR, QUAD = range(2), range(4)
HOPS = QUAD[1:]
ROW0, ROW1, ROW2 = (slice(i, i + 1) for i in range(3))
NT = (((1,), (1,)), ((), ()))
FIRST, LATER = ((1, 0), (2, 1)), ((1, 1), (2, 0))
DELTA = (0, 3, 1, 2)
SLOT = [DELTA.index(d) for d in QUAD]


def span(i, n):
    return slice(i * n, i * n + n)


def sum4(buf):
    return (buf[0] + buf[1]) + (buf[2] + buf[3])


def two(n):
    return lax.rem(n, 2)


def four(n):
    return lax.rem(n, 4)


def side(i):
    return 1 + 2 * i


def remote(src, dst, send, recv, where):
    return pltpu.make_async_remote_copy(src_ref=src, dst_ref=dst, send_sem=send, recv_sem=recv, device_id=where, device_id_type=MESH)


def forward_kernel(
    h_ref, ge_ref, w_ref, ints_ref, et_ref,
    logit_ref, zb_out, uf_out, gf_out, row_ref, ids_ref, aux_ref,
    e_s, stage, ebuf, uf, zb, ints, stats, ny, nz,
    esem, osem, zsem, fsem, usend, urecv, psend, precv, isend, irecv, ssend, srecv, nsend, nrecv,
):
    core = lax.axis_index("tp")
    xi, yi, zi = lax.axis_index("x"), lax.axis_index("y"), lax.axis_index("z")
    other = 1 - core

    def at_x(d):
        return four(xi + d)

    right, left = at_x(1), at_x(3)
    vstart = xi * VB

    def ecopy(i, slot):
        cols = pl.ds(pl.multiple_of(vstart + i * EC, LANE), EC)
        return pltpu.make_async_copy(et_ref.at[:, cols], ebuf.at[slot], esem.at[slot])

    ecopy(0, 0).start()
    barrier = pltpu.get_barrier_semaphore()
    peers = [{"x": at_x(d)} for d in HOPS] + [{"x": at_x(d), "tp": other} for d in QUAD]
    peers += [{"y": four(yi + d)} for d in HOPS] + [{"z": four(zi + d)} for d in HOPS]
    for peer in peers:
        pl.semaphore_signal(barrier, inc=1, device_id=peer, device_id_type=MESH)

    ints[0] = ints_ref[...]
    weight = w_ref[...].astype(F32)
    for half in PAIR:
        for q in PAIR:
            lo = half * TS + q * TB
            rows = h_ref[:, lo:lo + TB].astype(F32)
            inv = lax.rsqrt(jnp.mean(rows * rows, axis=0, keepdims=True) + RMS_EPS)
            uf[half, q] = rows * inv
    for q in PAIR:
        lo = q * TB
        gf_out[q] = jnp.where(core == 0, ge_ref[:, lo:lo + TB].astype(F32), ge_ref[:, TS + lo:TS + lo + TB].astype(F32))
    pl.semaphore_wait(barrier, len(peers))

    def ucopy(src, q, dst, way, index):
        return remote(uf.at[2 * src + core, q], uf.at[2 * dst + core, q], usend.at[index], urecv.at[dst, q], {"x": way})

    def pcopy(r, q):
        return remote(uf.at[2 * r + core, q], uf.at[2 * r + core, q], psend.at[r, q], precv.at[r, q], {"tp": other})

    def parrive(r, q):
        return remote(uf.at[2 * r + core, q], uf.at[2 * r + other, q], psend.at[r, q], precv.at[r, q], {"tp": other})

    ways = (left, right)
    own = [ucopy(0, q, r, ways[r % 2], i) for i, (r, q) in enumerate(FIRST + LATER)]
    onward = [ucopy(r, q, 3, ways[r % 2], 4 + q) for r, q in FIRST]

    def icopy(d):
        return remote(ints.at[0], ints.at[SLOT[-d % 4]], isend.at[d], irecv.at[SLOT[-d % 4]], {"x": at_x(d)})

    for copy in own[:2]:
        copy.start()
    for d in HOPS:
        icopy(d).start()
    for copy in own[2:]:
        copy.start()

    def ebody(i, _):
        slot = two(i)

        @pl.when(i + 1 < VB // EC)
        def _():
            ecopy(i + 1, 1 - slot).start()

        ecopy(i, slot).wait()
        e_s[pl.ds(pl.multiple_of(i * EC, EC), EC), :] = ebuf[slot].T
        return 0

    lax.fori_loop(0, VB // EC, ebody, 0)

    def scopy(r, d, cross):
        index = 2 * d + cross
        where = {"x": at_x(d), "tp": other} if cross else {"x": at_x(d)}
        dst = SLOT[(DELTA[r] - d) % 4]
        return remote(stats.at[0, r], stats.at[index, dst], ssend.at[index, r], srecv.at[index, dst], where)

    def stat_copies(r):
        return [scopy(r, d, cross) for d, cross in GROUP]

    def ncopy(buf, axis, me, d):
        k = {"y": 0, "z": 1}[axis]
        return remote(buf.at[me], buf.at[me], nsend.at[k, d], nrecv.at[k, d], {axis: four(me + d)})

    def narrive(buf, axis, me, d):
        k = {"y": 0, "z": 1}[axis]
        return remote(buf.at[me], buf.at[four(me + 4 - d)], nsend.at[k, d], nrecv.at[k, d], {axis: four(me + d)})

    iota = lax.broadcasted_iota(I32, (8, TB), 0)

    def ocopy(ts, q, slot):
        return pltpu.make_async_copy(stage.at[slot], logit_ref.at[ts, :, pl.ds(pl.multiple_of(q * TB, TB), TB)], osem.at[slot])

    def zcopy(ts, q):
        return pltpu.make_async_copy(zb.at[ts, q], zb_out.at[ts, q], zsem.at[ts, q])

    def fcopy(ts, q):
        return pltpu.make_async_copy(uf.at[ts, q], uf_out.at[ts, q], fsem.at[ts, q])

    def step(s, _):
        j = four(s)
        r = jnp.where(s < 4, 0, jnp.where(s < 12, 1 + two(j), 3))
        q = jnp.where((s < 8) | (s >= 12), two(j), 1 - two(j))
        half = jnp.where(s < 4, j // 2, jnp.where(j < 2, core, other))
        ts = 2 * r + half

        @pl.when(s == 4)
        def _():
            for i, (r, q) in enumerate(FIRST):
                own[i].wait_recv()
                onward[i].start()
                pcopy(r, q).start()
            for d in HOPS:
                icopy(d).wait_recv()
            for copy in stat_copies(0):
                copy.start()

        @pl.when(s == 6)
        def _():
            for r, q in FIRST:
                parrive(r, q).wait_recv()

        @pl.when(s == 8)
        def _():
            for i, (r, q) in enumerate(LATER):
                own[2 + i].wait_recv()
                pcopy(r, q).start()
            count = jnp.sum(ints[:, :, :, 2, :].astype(F32))
            ny[yi] = jnp.full((8, LANE), count, F32)
            for d in HOPS:
                ncopy(ny, "y", yi, d).start()

        @pl.when(s == 10)
        def _():
            for r, q in LATER:
                parrive(r, q).wait_recv()
            for d in HOPS:
                narrive(ny, "y", yi, d).wait_recv()
            nz[zi] = sum4(ny)
            for d in HOPS:
                ncopy(nz, "z", zi, d).start()

        @pl.when(s == 12)
        def _():
            for i in PAIR:
                onward[i].wait_recv()
                pcopy(3, i).start()
            for copy in stat_copies(1) + stat_copies(2):
                copy.start()

        @pl.when(s == 14)
        def _():
            for i in PAIR:
                parrive(3, i).wait_recv()

        slot = two(s)

        @pl.when(s >= 2)
        def _():
            ocopy(ts, q, slot).wait()

        zt = (uf[ts, q] * weight).astype(BF16)
        zb[ts, q] = zt
        zcopy(ts, q).start()
        fcopy(ts, q).start()
        tgt = ints[r, half, q, ROW0, :] - vstart
        m8 = jnp.full((8, TB), -jnp.inf, F32)
        s8 = jnp.zeros((8, TB), F32)
        t8 = jnp.zeros((8, TB), F32)
        for vc in range(VB // CH):
            l = jnp.dot(e_s[vc * CH:(vc + 1) * CH, :], zt, preferred_element_type=F32)
            stage[slot, vc * CH:(vc + 1) * CH, :] = l
            mn = m8
            for i in range(CH // 8):
                mn = jnp.maximum(mn, l[span(i, 8)])
            s8 = s8 * jnp.exp(m8 - mn)
            m8 = mn
            for i in range(CH // 8):
                li = l[span(i, 8)]
                s8 = s8 + jnp.exp(li - mn)
                t8 = t8 + jnp.where(iota == tgt - (vc * CH + i * 8), li, 0.0)
        m = jnp.max(m8, axis=0, keepdims=True)
        stats[0, r, half, q, ROW0, :] = m
        stats[0, r, half, q, ROW1, :] = jnp.sum(s8 * jnp.exp(m8 - m), axis=0, keepdims=True)
        stats[0, r, half, q, ROW2, :] = jnp.sum(t8, axis=0, keepdims=True)
        ocopy(ts, q, slot).start()
        return 0

    lax.fori_loop(0, 16, step, 0)
    for copy in stat_copies(3):
        copy.start()
    for d in HOPS:
        narrive(nz, "z", zi, d).wait_recv()
    total = sum4(nz)[ROW0, ROW0]
    for r in QUAD:
        for copy in stat_copies(r):
            copy.wait_recv()
    loss = jnp.zeros((1, TB), F32)
    for r in QUAD:
        for half in PAIR:
            for q in PAIR:
                lanes = span(q, TB)
                ms = [stats[i, r, half, q, ROW0, :] for i in range(8)]
                m = functools.reduce(jnp.maximum, ms)
                tot = sum(stats[i, r, half, q, ROW1, :] * jnp.exp(ms[i] - m) for i in range(8))
                tgt_logit = sum(stats[i, r, half, q, ROW2, :] for i in range(8))
                lse = m + jnp.log(tot)
                mask = ints[r, half, q, ROW2, :].astype(F32)
                row_ref[2 * r + half, ROW0, lanes] = lse
                row_ref[2 * r + half, ROW1, lanes] = mask / total
                ids_ref[2 * r + half, ROW0, lanes] = ints[r, half, q, ROW0, :] - vstart
                ids_ref[2 * r + half, ROW1, lanes] = ints[r, half, q, ROW1, :] - vstart
                if r == 0:
                    loss = loss + jnp.where(core == half, mask * (lse - tgt_logit), 0.0)
    aux_ref[...] = jnp.zeros_like(aux_ref)
    aux_ref[ROW0, :] = jnp.broadcast_to(jnp.sum(loss, axis=1, keepdims=True), (1, LANE))
    aux_ref[ROW1, :] = jnp.broadcast_to(total, (1, LANE))
    for copy in own + onward:
        copy.wait_send()
    for r in HOPS:
        for q in PAIR:
            pcopy(r, q).wait_send()
    for d in HOPS:
        icopy(d).wait_send()
        ncopy(ny, "y", yi, d).wait_send()
        ncopy(nz, "z", zi, d).wait_send()
    for r in QUAD:
        for copy in stat_copies(r):
            copy.wait_send()
    for slot in PAIR:
        ocopy(0, 0, slot).wait()
    for ts in range(NS):
        for q in PAIR:
            zcopy(ts, q).wait()
            fcopy(ts, q).wait()


def forward(h_t, ge_t, w, ints, et):
    return pl.pallas_call(
        forward_kernel,
        out_shape=(
            SDS((NS, VB, TS), F32),
            SDS(TOKENS, BF16),
            SDS(TOKENS, F32),
            SDS(TOKENS[1:], F32),
            SDS((NS, SUB, TS), F32),
            SDS((NS, SUB, TS), I32),
            SDS((SUB, LANE), F32),
        ),
        in_specs=[VMEM] * 4 + [ANY],
        out_specs=(ANY,) * 3 + (VMEM,) * 4,
        scratch_shapes=[
            V((VB, D), BF16),
            V((2, VB, TB), F32),
            V((2, D, EC), BF16),
            V(TOKENS, F32),
            V(TOKENS, BF16),
            V((GX, 2, 2, SUB, TB), I32),
            V((NS, GX, 2, 2, SUB, TB), F32),
            *[V((GX, SUB, LANE), F32)] * 2,
            *[DMA((2,))] * 2, *[DMA((NS, 2))] * 2, DMA((NS,)), *[DMA((GX, 2))] * 3,
            *[DMA((GX,))] * 2, *[DMA((NS, GX))] * 2, *[DMA((2, GX))] * 2,
        ],
        compiler_params=pltpu.CompilerParams(vmem_limit_bytes=62 << 20, collective_id=0, has_side_effects=True),
    )(h_t, ge_t, w, ints, et)


NP = 6
NA = 16


def backward_kernel(
    et_ref, zb_ref, row_ref, ids_ref, logit_ref, gf_ref, uf_ref, ge_ref, h_ref, w_ref, aux_ref,
    de_out, dh_out, sum_out, gall,
    gb, dz, de, lbuf, et_s, gst, ra1, ra2, rb1, rb2, fin, sb, rv, dzp, rc1, rc2, hbuf, st, sx, sy, sz,
    lsem, esem, gsem, gown, hsem, gsend, grecv, gpsend, gprecv,
    a1s, a1r, a2s, a2r, b1s, b1r, b2s, b2r, ass, asr, dps, dpr, c1s, c1r, c2s, c2r, hs, hr, sts, str_, sas, sar,
):
    core = lax.axis_index("tp")
    xi, yi, zi = lax.axis_index("x"), lax.axis_index("y"), lax.axis_index("z")
    other = 1 - core
    me = {"x": xi, "y": yi, "z": zi}

    def at(axis, d):
        return four(me[axis] + d)

    right, left = at("x", 1), at("x", 3)
    vstart = xi * VB
    iota = lax.broadcasted_iota(I32, (V2, TS), 0)

    def lcopy(vc, slot):
        return pltpu.make_async_copy(logit_ref.at[:, pl.ds(pl.multiple_of(vc * V2, V2), V2), :], lbuf.at[slot], lsem.at[slot])

    def ecopy(vc, slot):
        cols = pl.ds(pl.multiple_of(vstart + vc * V2, LANE), V2)
        return pltpu.make_async_copy(et_ref.at[:, cols], et_s.at[slot], esem.at[slot])

    for slot in PAIR:
        lcopy(slot, slot).start()
        ecopy(slot, slot).start()
    barrier = pltpu.get_barrier_semaphore()
    peers = [{"y": at("y", dy), "x": at("x", dx)} for dy, dx in FAR]
    peers += [{"z": at("z", d)} for d in HOPS] + [{"tp": other}]
    for peer in peers:
        pl.semaphore_signal(barrier, inc=1, device_id=peer, device_id_type=MESH)
    pl.semaphore_wait(barrier, len(peers))

    def gcopy(q, dst, way, index):
        return remote(gf_ref.at[q], gall.at[2 * dst + core, q], gsend.at[index], grecv.at[dst, q], {"x": way})

    def gonward(src, q, way, index):
        return remote(gall.at[2 * src + core, q], gall.at[6 + core, q], gsend.at[index], grecv.at[3, q], {"x": way})

    def gpcopy(r, q):
        return remote(gall.at[2 * r + core, q], gall.at[2 * r + core, q], gpsend.at[r, q], gprecv.at[r, q], {"tp": other})

    def gparrive(r, q):
        return remote(gall.at[2 * r + core, q], gall.at[2 * r + other, q], gpsend.at[r, q], gprecv.at[r, q], {"tp": other})

    ways = (left, right)
    gown_copies = [gcopy(q, r, ways[r % 2], i) for i, (r, q) in enumerate(FIRST + LATER)]
    gonward_copies = [gonward(r, q, ways[r % 2], 4 + q) for r, q in FIRST]
    for copy in gown_copies:
        copy.start()

    def own_ge(half, q):
        return pltpu.make_async_copy(ge_ref.at[:, pl.ds(half * TS + q * TB, TB)], gb.at[half, q], gown.at[half, q])

    for half in PAIR:
        for q in PAIR:
            own_ge(half, q).start()
    hcopy = pltpu.make_async_copy(h_ref.at[:, pl.ds(pl.multiple_of(core * TS, TS), TS)], hbuf, hsem)
    hcopy.start()

    def piece(p):
        third = p >= 8
        hi = two(p // 2)
        r = jnp.where(third, 3, 1 + hi)
        q = jnp.where(third, hi, jnp.where(p < 4, hi, 1 - hi))
        return 2 * r + two(p), q

    def stage_in(p):
        ts, q = piece(p)
        return pltpu.make_async_copy(gall.at[ts, q], gst.at[two(p)], gsem.at[two(p)])

    def convert(p):
        ts, q = piece(p)
        stage_in(p).wait()
        gb[ts, q] = gst[two(p)].astype(BF16)

    dz[...] = jnp.zeros_like(dz)

    def de_index(u, zblk, qtr):
        return jnp.where(two(u) == 0, zblk * 4 + qtr, qtr * 4 + zblk)

    def logits_step(vc):
        slot = two(vc)
        lcopy(vc, slot).wait()
        ecopy(vc, slot).wait()
        et = et_s[slot]
        base = vc * V2
        acc = None
        for ts in range(NS):
            r, half = ts // 2, ts % 2
            p = jnp.exp(lbuf[slot, ts] - row_ref[ts, ROW0, :])
            d = (jnp.where(iota == ids_ref[ts, ROW0, :] - base, p - 1.0, p) * row_ref[ts, ROW1, :]).astype(BF16)
            dz[half, r] += jnp.dot(et, d, preferred_element_type=F32)
            for q in PAIR:
                a = lax.dot_general(zb_ref[ts, q], d[:, span(q, TB)], NT, preferred_element_type=F32)
                acc = a if acc is None else acc + a
        u = vc // 2
        for zblk in QUAD:
            for ql in PAIR:
                de[u, de_index(u, zblk, slot * 2 + ql)] = acc[span(zblk, ROWS), span(ql, LANE)]
        nxt = jnp.minimum(vc + 2, N2 - 1)
        lcopy(nxt, slot).start()
        ecopy(nxt, slot).start()

    def lookup_step(vc):
        base = vc * V2
        acc = None
        for ts in range(NS):
            o = jnp.where(iota == ids_ref[ts, ROW1, :] - base, 1.0, 0.0).astype(BF16)
            for q in PAIR:
                a = lax.dot_general(gb[ts, q], o[:, span(q, TB)], NT, preferred_element_type=F32)
                acc = a if acc is None else acc + a
        u = vc // 2
        for zblk in QUAD:
            for ql in PAIR:
                de[u, de_index(u, zblk, two(vc) * 2 + ql)] += acc[span(zblk, ROWS), span(ql, LANE)]

    AXES = ("zy", "yz")

    def hop(axis, i):
        return {axis: at(axis, side(i))}

    def a1(p, c):
        a, _ = AXES[c]
        k, op = two(p), at(a, 2) * 4
        return [remote(de.at[2 * p + c, pl.ds(op + 2 * i, 2)], ra1.at[c, k, i], a1s.at[c, k, i], a1r.at[c, k, i], hop(a, i)) for i in PAIR]

    def a2(p, c):
        a, _ = AXES[c]
        k = two(p)
        return [remote(de.at[2 * p + c, pl.ds(at(a, side(i)) * 4, 4)], ra2.at[c, k, i], a2s.at[c, k, i], a2r.at[c, k, i], hop(a, i)) for i in PAIR]

    def b1(p, c):
        a, b = AXES[c]
        k, i2 = two(p), me[a] * 4 + at(b, 2)
        return [remote(de.at[2 * p + c, i2, pl.ds(HROWS * i, HROWS)], rb1.at[c, k, i], b1s.at[c, k, i], b1r.at[c, k, i], hop(b, i)) for i in PAIR]

    def b2(p, c):
        a, b = AXES[c]
        k = two(p)
        return [remote(de.at[2 * p + c, me[a] * 4 + at(b, side(i))], rb2.at[c, k, i], b2s.at[c, k, i], b2r.at[c, k, i], hop(b, i)) for i in PAIR]

    def start(copies):
        for copy in copies:
            copy.start()

    def wait(copies):
        for copy in copies:
            copy.wait()

    def do_a1(p):
        for c in PAIR:
            start(a1(p, c))

    def do_a2(p):
        k = two(p)
        for c in PAIR:
            a, _ = AXES[c]
            wait(a1(p, c))
            for i in PAIR:
                for j in PAIR:
                    de[2 * p + c, at(a, side(i)) * 4 + 2 * i + j] += ra1[c, k, i, j]
            start(a2(p, c))

    def do_b1(p):
        k = two(p)
        for c in PAIR:
            a, _ = AXES[c]
            wait(a2(p, c))
            for j in QUAD:
                de[2 * p + c, me[a] * 4 + j] += ra2[c, k, 0, j] + ra2[c, k, 1, j]
            start(b1(p, c))

    def do_b2(p):
        k = two(p)
        for c in PAIR:
            a, b = AXES[c]
            wait(b1(p, c))
            for i in PAIR:
                de[2 * p + c, me[a] * 4 + at(b, side(i)), span(i, HROWS)] += rb1[c, k, i]
            start(b2(p, c))

    def do_f(p):
        k = two(p)
        for c in PAIR:
            a, b = AXES[c]
            wait(b2(p, c))
            fin[2 * p + c] = de[2 * p + c, me[a] * 4 + me[b]] + rb2[c, k, 0] + rb2[c, k, 1]

    def col(b, dy, dx):
        dst = at("y", dy) * 4 + at("x", dx)
        return remote(sb.at[b, dst], rv.at[b, yi * 4 + xi], ass.at[b, dy * 4 + dx], asr.at[b, dy * 4 + dx], {"y": at("y", dy), "x": at("x", dx)})

    def col_arrive(b, dy, dx):
        src = at("y", 4 - dy) * 4 + at("x", 4 - dx)
        return remote(sb.at[b, src], rv.at[b, src], ass.at[b, dy * 4 + dx], asr.at[b, dy * 4 + dx], {"y": at("y", dy), "x": at("x", dx)})

    def do_cols(b):
        for s in range(16):
            for k in range(6):
                sb[b, s, span(k, OWN), :] = fin[6 * b + k, span(s, OWN), :]
        for dy, dx in FAR:
            col(b, dy, dx).start()
        rv[b, yi * 4 + xi] = sb[b, yi * 4 + xi]

    def do_assemble(b):
        for dy, dx in FAR:
            col_arrive(b, dy, dx).wait_recv()
        for s in range(16):
            for k in range(6):
                lane = (s % 4) * VB + (6 * b + k) * EC + (s // 4) * LANE
                de_out[:, lane:lane + LANE] = rv[b, s, span(k, OWN), :]

    def phase_a(vc, _):
        @pl.when(vc == 6)
        def _():
            for i, (r, q) in enumerate(FIRST):
                gown_copies[i].wait_recv()
                gonward_copies[i].start()
                gpcopy(r, q).start()

        @pl.when(vc == 7)
        def _():
            for r, q in FIRST:
                gparrive(r, q).wait_recv()

        @pl.when(vc == 10)
        def _():
            for i, (r, q) in enumerate(LATER):
                gown_copies[2 + i].wait_recv()
                gpcopy(r, q).start()

        @pl.when(vc == 11)
        def _():
            for r, q in LATER:
                gparrive(r, q).wait_recv()

        @pl.when(vc >= 8)
        def _():
            convert(vc - 8)

        @pl.when((vc >= 7) & (vc < 15))
        def _():
            stage_in(vc - 7).start()

        logits_step(vc)
        return 0

    lax.fori_loop(0, NA, phase_a, 0)
    for i in PAIR:
        gonward_copies[i].wait_recv()
        gpcopy(3, i).start()
    for i in PAIR:
        gparrive(3, i).wait_recv()
    for half in PAIR:
        for q in PAIR:
            own_ge(half, q).wait()
    stage_in(8).start()
    for p in range(8, 12):
        if p < 11:
            stage_in(p + 1).start()
        convert(p)

    def phase_c(p, _):
        def lookups(i, _):
            lookup_step(4 * p + i)
            return 0

        lax.fori_loop(0, 4, lookups, 0)
        do_a1(p)

        @pl.when(p >= 2)
        def _():
            do_b2(p - 2)

        def more(i, _):
            logits_step(NA + 2 * p + i)
            return 0

        lax.fori_loop(0, 2, more, 0)
        do_a2(p)

        @pl.when(p >= 1)
        def _():
            do_b1(p - 1)

        @pl.when(p >= 2)
        def _():
            do_f(p - 2)

        return 0

    lax.fori_loop(0, 4, phase_c, 0)
    for slot in PAIR:
        lcopy(N2 - 1, slot).wait()
        ecopy(N2 - 1, slot).wait()

    def dcopy(r):
        return remote(dz.at[other, r], dzp.at[r], dps.at[r], dpr.at[r], {"tp": other})

    for r in (3, 1, 2, 0):
        dcopy(r).start()

    def ucopy(i):
        return pltpu.make_async_copy(uf_ref.at[i // 2, i % 2], gst.at[i % 2], gsem.at[i % 2])

    ucopy(0).start()
    total = jnp.zeros((D, LANE), F32)
    for i in range(16):
        if i < 15:
            ucopy(i + 1).start()
        ucopy(i).wait()
        r, half, q = i // 4, (i // 2) % 2, i % 2
        for j in PAIR:
            lo = q * TB + LANE * j
            total = total + dz[half, r, :, lo:lo + LANE] * gst[i % 2, :, span(j, LANE)]
    dg = jnp.sum(total.T, axis=0, keepdims=True)

    def sum_start(buf, axis):
        k = {"x": 0, "y": 1, "z": 2}[axis]
        for d in HOPS:
            remote(buf.at[me[axis]], buf.at[me[axis]], sas.at[k, d], sar.at[k, d], {axis: at(axis, d)}).start()

    def sum_wait(buf, axis):
        k = {"x": 0, "y": 1, "z": 2}[axis]
        for d in HOPS:
            remote(buf.at[me[axis]], buf.at[at(axis, 4 - d)], sas.at[k, d], sar.at[k, d], {axis: at(axis, d)}).wait()
        return sum4(buf)

    st[core] = jnp.zeros((8, 640), F32)
    st[core, 0:1, 0:D] = dg
    st[core, 1:2, 0:LANE] = aux_ref[ROW0, :]
    pair_copy = remote(st.at[core], st.at[core], sts, str_, {"tp": other})
    pair_arrive = remote(st.at[core], st.at[other], sts, str_, {"tp": other})
    def dz_add(r):
        dcopy(r).wait_recv()
        dz[core, r] += dzp[r]

    def c1(i):
        return remote(dz.at[core, 3, pl.ds(HD * i, HD)], rc1.at[i], c1s.at[i], c1r.at[i], hop("x", i))

    def c2(i):
        return remote(dz.at[core, 2 - i], rc2.at[i], c2s.at[i], c2r.at[i], hop("x", i))

    dz_add(3)
    for i in PAIR:
        c1(i).start()
    pair_copy.start()

    def lookups4(i, _):
        lookup_step(16 + i)
        return 0

    lax.fori_loop(0, 4, lookups4, 0)
    do_a1(4)
    do_b2(2)
    pair_arrive.wait()
    sx[xi] = st[0] + st[1]
    sum_start(sx, "x")
    dz_add(1)
    dz_add(2)
    do_b1(3)
    do_f(2)
    do_cols(0)

    def lookups5(i, _):
        lookup_step(20 + i)
        return 0

    lax.fori_loop(0, 4, lookups5, 0)
    do_a1(5)
    do_a2(4)
    do_b2(3)
    sy[yi] = sum_wait(sx, "x")
    sum_start(sy, "y")
    for i in PAIR:
        c1(i).wait()
        dz[core, 2 - i, span(i, HD)] += rc1[i]
        c2(i).start()
    dz_add(0)
    do_a2(5)
    sz[zi] = sum_wait(sy, "y")
    sum_start(sz, "z")
    do_f(3)
    do_b1(4)
    do_assemble(0)
    do_b2(4)
    do_b1(5)
    do_f(4)
    do_b2(5)
    sum_out[...] = sum_wait(sz, "z")
    do_f(5)
    do_cols(1)

    hcopy.wait()
    rows = hbuf[...].astype(F32)
    inv = lax.rsqrt(jnp.mean(rows * rows, axis=0, keepdims=True) + RMS_EPS)
    unit = rows * inv
    for i in PAIR:
        c2(i).wait()
    gu = (dz[core, 0] + rc2[0] + rc2[1]) * w_ref[...].astype(F32)
    dz[core, 3] = inv * (gu - unit * jnp.mean(gu * unit, axis=0, keepdims=True))
    half_copy = remote(dz.at[core, 3], dzp.at[3], hs, hr, {"tp": other})
    half_copy.start()
    do_assemble(1)
    half_copy.wait()
    for half in PAIR:
        dh_out[:, span(half, TS)] = jnp.where(core == half, dz[core, 3], dzp[3]).astype(BF16)

    for copy in gown_copies + gonward_copies:
        copy.wait_send()
    for r in HOPS:
        for q in PAIR:
            gpcopy(r, q).wait_send()
    for r in QUAD:
        dcopy(r).wait_send()
    for b in PAIR:
        for dy, dx in FAR:
            col(b, dy, dx).wait_send()


def backward(et, zb, row, ids, logit, gf, uf, ge_t, h_t, w, aux):
    return pl.pallas_call(
        backward_kernel,
        out_shape=(SDS((OWN, VL), F32), SDS((D, TOK), BF16), SDS(SUMS, F32), SDS(TOKENS, F32)),
        in_specs=[ANY] + [VMEM] * 3 + [ANY] * 5 + [VMEM] * 2,
        out_specs=(VMEM,) * 3 + (ANY,),
        scratch_shapes=[
            V(TOKENS, BF16),
            V((2, GX, D, TS), F32),
            V((2 * NP, 16, ROWS, LANE), F32),
            V((2, NS, V2, TS), F32),
            V((2, D, V2), BF16),
            V((2, D, TB), F32),
            V((2, 2, 2, 2, ROWS, LANE), F32),
            V((2, 2, 2, GX, ROWS, LANE), F32),
            V((2, 2, 2, HROWS, LANE), F32),
            V((2, 2, 2, ROWS, LANE), F32),
            V((2 * NP, ROWS, LANE), F32),
            *[V((2, 16, 56, LANE), F32)] * 2,
            V((GX, D, TS), F32),
            V((2, HD, TS), F32),
            V((2, D, TS), F32),
            V((D, TS), BF16),
            V((2, *SUMS), F32), *[V((GX, *SUMS), F32)] * 3,
            *[DMA((2,))] * 3, DMA((2, 2)), DMA(()), DMA((NS,)), *[DMA((GX, 2))] * 3,
            *[DMA((2, 2, 2))] * 8,
            *[DMA((2, 16))] * 2, *[DMA((GX,))] * 2, *[DMA((2,))] * 4, *[DMA(())] * 4, *[DMA((3, GX))] * 2,
        ],
        compiler_params=pltpu.CompilerParams(vmem_limit_bytes=67043328, collective_id=1, has_side_effects=True),
    )(et, zb, row, ids, logit, gf, uf, ge_t, h_t, w, aux)


def solution(mesh):
    mesh4 = Mesh(mesh.devices.reshape(2, 4, 4, 4), ("tp", "z", "y", "x"))

    def local_step(hidden, norm_w, embed, targets, loss_mask, token_ids, grad_embed):
        core = lax.axis_index("tp")
        h_t = hidden.reshape(TOK, D).T
        ge_t = grad_embed.reshape(TOK, D).T
        et = embed.T
        w = norm_w.reshape(D, 1)
        base = core * VL
        own = [a.reshape(2, 2, 1, TB) for a in (targets - base, token_ids - base, loss_mask)]
        ints = jnp.concatenate(own + own[:1] * 5, axis=2)
        logit, zb, uf, gf, row, ids, aux = forward(h_t, ge_t, w, ints, et)
        de, dh, sums, _ = backward(et, zb, row, ids, logit, gf, uf, ge_t, h_t, w, aux)
        loss_val = sums[1, 0] / aux[1, 0]
        return loss_val, dh.T.reshape(1, TOK, D), sums[0, :D], de.T

    dp = ("z", "y", "x")
    return jax.shard_map(
        local_step,
        mesh=mesh4,
        in_specs=(P(dp), P(), P("tp"), P(dp), P(dp), P(dp), P(dp)),
        out_specs=(P(), P(dp), P(), P("tp", dp)),
        check_vma=False,
    )
```

time: 627 us -> 269 us (0.43)
  waiting for transfers between devices: 201 us -> 0 us
  local copies, waits for them, and re-layouts: 116 us -> 10.2 us
  blocking collectives: 66.7 us -> 0 us
  Pallas kernels: 188 us -> 252 us
  other arithmetic: 25.1 us -> 0.71 us
  between operations: 16.8 us -> 3.13 us
  starting transfers between devices: 8.96 us -> 0 us
    unnamed x5 -> x0, waiting for transfers between devices: 96.1 us -> none
    psum x1 -> x0, blocking collectives: 66.7 us -> none  [local_step(): loss_val = lax.psum(aux[0, 0], ('tp', 'z', 'y', 'x')) / aux[1, 0]]
    pallas_call x2, Pallas kernels: 188 us -> 252 us  [the longest x1 180 us: backward(): pl.pallas_call(backward_kernel, out_shape=(SDS((OWN, VL), F32), SDS((D, T...]
    all_gather x1 -> x0, waiting for transfers between devices: 47.9 us -> none  [local_step(): gg = lax.all_gather(gf, ('x', 'tp'), axis=0)]
    reshape x7 -> x1, local copies, waits for them, and re-layouts: 43.3 us -> 1.49 us  [local_step(): w = norm_w.reshape(D, 1)]
    reduce_scatter x1 -> x0, waiting for transfers between devices: 39 us -> none  [local_step(): dz = lax.psum_scatter(dz, 'x', scatter_dimension=0, tiled=True)]
    transpose x3 -> x0, local copies, waits for them, and re-layouts: 33 us -> none  [the longest x2 32.9 us: local_step(): de = de.transpose(1, 0, 2).reshape(D, 16, VB // 16).transpose(1, 0, 2)]
    psum x1 -> x0, waiting for transfers between devices: 18.2 us -> none  [local_step(): dz = lax.psum(dz, 'tp').reshape(2, D, TS).transpose(1, 0, 2).reshape(D, TOK)]
  transfers between devices with their start and end apart: 5 -> 0, of which waited for: 4 -> 0; matrix products, arithmetic and copies ran while one was open for 11% -> 0% of each run, Pallas kernels for 0% -> 0%
where the time goes in v3:
time: 269 us; the launch traced here: 266 us
  Pallas kernels  252 us (94%)
  local copies, waits for them, and re-layouts  10.2 us (4%)
  between operations  3.13 us (1%)
    pallas_call x1, Pallas kernels, backward(): pl.pallas_call(backward_kernel, out_shape=(SDS((OWN, VL), F32), SDS((D, T...  180 us
    pallas_call x1, Pallas kernels, forward(): pl.pallas_call(forward_kernel, out_shape=(SDS((NS, VB, TS), F32), SDS(TOK...  72 us

profile of v3, /device:TPU:1, one launch (start us, length us, event | category | flops | bytes accessed | tf_op | source)
XLA Modules:
  0.0 266.3 jit_solution(1692650625237486715)
XLA Ops:
  0.6 0.7 broadcast_subtract_fusion
  1.3 1.4 concatenate.3.ints_ref
  2.7 1.5 reshape.37.w_ref
  4.2 72.0 %shard_map.102 = (f32[8,6144,512]{2,1,0:T(8,128)}, bf16[8,2,576,256]{3,2,1,0:T(8,128)(2,1)}, f32[8,2,576,256]{3,2,1,0:T(8,128)}, f32[2,576,256]{2,1,0:T(8,128)},...) custom-call(bf16[576,1024]{1,0:T(8,128)(2,1)} %bitcast.17, bf16[576,1024]{1,0:T(8,128)(2,1)} %bitcast.19, ...), custom_call_target="tpu_custom_call" | custom-call | tf_op jit(solution)/shard_map/pallas_call | solution.py:311
  76.2 180.2 %shard_map.103 = (f32[9,24576]{1,0:T(8,128)}, bf16[576,1024]{1,0:T(8,128)(2,1)}, f32[8,640]{1,0:T(8,128)}, f32[8,2,576,256]{3,2,1,0:T(8,128)}) custom-call(bf16[576,24576]{1,0:T(8,128)(2,1)} %bitcast.16, bf16[8,2,576,256]{3,2,1,0:T(8,128)(2,1)} %get-tuple-element.14.zb_ref, f32[8,8,512]{2,1,0:T(8,128)} %get-tuple-element.15.row_ref, ...), custom_call_target="tpu_custom_call" | custom-call | tf_op jit(solution)/shard_map/pallas_call | solution.py:769
  256.4 0.0 copy-start
  256.4 1.4 slice_reduce_fusion
  257.9 1.2 slice.9
  259.1 1.2 slice.10
  261.6 2.4 copy.15
  264.0 0.0 copy-done
  264.0 1.1 copy.16
Async XLA Ops:
  256.4 7.5 %copy-start = (f32[9,24576]{1,0:T(8,128)S(1)}, f32[9,24576]{1,0:T(8,128)}, u32[]{:S(2)}) copy-start(f32[9,24576]{1,0:T(8,128)} %get-tuple-element.23) | copy-start | bytes 2654212

commit v4 on v0

v4 whole, which is shorter than its diff:
```python
import functools

import jax
import jax.numpy as jnp
from jax import lax
from jax.experimental import pallas as pl
from jax.experimental.pallas import tpu as pltpu
from jax.sharding import Mesh, PartitionSpec as P

RMS_EPS = 1e-6
F32, BF16, I32 = jnp.float32, jnp.bfloat16, jnp.int32
MESH = pl.DeviceIdType.MESH
D = 576
TOK = 1024
GX = 4
VL = 24576
VB = VL // GX
TS = 512
TB = 256
NS = GX * 2
V2 = 256
N2 = VB // V2
CH = 256
ROWS, LANE, OWN = 144, 128, 9
HROWS, HD, EC = ROWS // 2, D // 2, 512
VMEM = pl.BlockSpec(memory_space=pltpu.VMEM)
ANY = pl.BlockSpec(memory_space=pl.ANY)
V, DMA, SDS = pltpu.VMEM, pltpu.SemaphoreType.DMA, jax.ShapeDtypeStruct
SUB = 8
TOKENS = (NS, 2, D, TB)
SUMS = (SUB, 640)
GRID = [(dy, dx) for dy in range(4) for dx in range(4)]
FAR = GRID[1:]
GROUP = [(d, cross) for d in range(4) for cross in range(2) if d or cross]
PAIR, QUAD = range(2), range(4)
HOPS = QUAD[1:]
ROW0, ROW1, ROW2 = (slice(i, i + 1) for i in range(3))
NT = (((1,), (1,)), ((), ()))
FIRST, LATER = ((1, 0), (2, 1)), ((1, 1), (2, 0))
DELTA = (0, 3, 1, 2)
SLOT = [DELTA.index(d) for d in QUAD]


def span(i, n):
    return slice(i * n, i * n + n)


def sum4(buf):
    return (buf[0] + buf[1]) + (buf[2] + buf[3])


def two(n):
    return lax.rem(n, 2)


def four(n):
    return lax.rem(n, 4)


def side(i):
    return 1 + 2 * i


def remote(src, dst, send, recv, where):
    return pltpu.make_async_remote_copy(src_ref=src, dst_ref=dst, send_sem=send, recv_sem=recv, device_id=where, device_id_type=MESH)


NP = 6
NA = 9
AXES = ("zy", "yz")


def kernel(
    h_ref, ge_ref, w_ref, ints_ref, et_ref,
    de_out, dh_out, sum_out, logit_ref, uf_out, gall,
    uf, zb, gb, gst, ints, stats, hits, ny, nz, row, ids, aux,
    ra1, ra2, rb1, rb2, sb, rv, st, sx, sy, sz,
    etsem, osem, lsem, esem, gsem, gown, zsem, fsem,
    usend, urecv, psend, precv, isend, irecv, ssend, srecv, nsend, nrecv,
    gsend, grecv, gpsend, gprecv, a1s, a1r, a2s, a2r, b1s, b1r, b2s, b2r,
    ass, asr, dps, dpr, c1s, c1r, c2s, c2r, hs, hr, sts, str_, sas, sar,
):
    core = lax.axis_index("tp")
    me = {axis: lax.axis_index(axis) for axis in "xyz"}
    xi, yi, zi = (me[axis] for axis in "xyz")
    other = 1 - core
    vstart = xi * VB

    def at(axis, d):
        return four(me[axis] + d)

    def hop(axis, i):
        return {axis: at(axis, side(i))}

    barrier = pltpu.get_barrier_semaphore()
    peers = [{"y": at("y", dy), "x": at("x", dx)} for dy, dx in FAR]
    peers += [{"z": at("z", d)} for d in HOPS] + [{"x": at("x", d), "tp": other} for d in QUAD]
    for peer in peers:
        pl.semaphore_signal(barrier, inc=1, device_id=peer, device_id_type=MESH)

    def start(copies):
        for copy in copies:
            copy.start()

    def wait(copies):
        for copy in copies:
            copy.wait()

    def arrive(copies):
        for copy in copies:
            copy.wait_recv()

    def sent(copies):
        for copy in copies:
            copy.wait_send()

    right, left = at("x", 1), at("x", 3)
    ways = (left, right)

    def ucopy(src, q, dst, way, index):
        return remote(uf.at[2 * src + core, q], uf.at[2 * dst + core, q], usend.at[index], urecv.at[dst, q], {"x": way})

    def pcopy(r, q):
        return remote(uf.at[2 * r + core, q], uf.at[2 * r + core, q], psend.at[r, q], precv.at[r, q], {"tp": other})

    def parrive(r, q):
        return remote(uf.at[2 * r + core, q], uf.at[2 * r + other, q], psend.at[r, q], precv.at[r, q], {"tp": other})

    own = [ucopy(0, q, r, ways[r % 2], i) for i, (r, q) in enumerate(FIRST + LATER)]
    onward = [ucopy(r, q, 3, ways[r % 2], 4 + q) for r, q in FIRST]

    def gcopy(src, q, dst, way, index):
        return remote(gall.at[2 * src + core, q], gall.at[2 * dst + core, q], gsend.at[index], grecv.at[dst, q], {"x": way})

    def gpcopy(r, q):
        return remote(gall.at[2 * r + core, q], gall.at[2 * r + core, q], gpsend.at[r, q], gprecv.at[r, q], {"tp": other})

    def gparrive(r, q):
        return remote(gall.at[2 * r + core, q], gall.at[2 * r + other, q], gpsend.at[r, q], gprecv.at[r, q], {"tp": other})

    gmine = [gcopy(0, q, r, ways[r % 2], i) for i, (r, q) in enumerate(FIRST + LATER)]
    gonward = [gcopy(r, q, 3, ways[r % 2], 4 + q) for r, q in FIRST]

    def own_ge(half, q):
        return pltpu.make_async_copy(ge_ref.at[:, pl.ds(half * TS + q * TB, TB)], gb.at[half, q], gown.at[half, q])

    def out_dh(half, q):
        return pltpu.make_async_copy(gb.at[half, q], dh_out.at[:, pl.ds(half * TS + q * TB, TB)], gown.at[half, q])

    def keep_ge(q):
        return pltpu.make_async_copy(gst.at[q], gall.at[core, q], gsem.at[q])

    def icopy(d):
        return remote(ints.at[0], ints.at[SLOT[-d % 4]], isend.at[d], irecv.at[SLOT[-d % 4]], {"x": at("x", d)})

    def scopy(r, d, cross):
        index = 2 * d + cross
        where = {"x": at("x", d), "tp": other} if cross else {"x": at("x", d)}
        dst = SLOT[(DELTA[r] - d) % 4]
        return remote(stats.at[0, r], stats.at[index, dst], ssend.at[index, r], srecv.at[index, dst], where)

    def stat_copies(r):
        return [scopy(r, d, cross) for d, cross in GROUP]

    def gather_axis(buf, axis, sends, recvs):
        mine = me[axis]
        out = [remote(buf.at[mine], buf.at[mine], sends.at[d], recvs.at[d], {axis: at(axis, d)}) for d in HOPS]
        back = [remote(buf.at[mine], buf.at[at(axis, -d % 4)], sends.at[d], recvs.at[d], {axis: at(axis, d)}) for d in HOPS]
        return out, back

    ny_out, ny_in = gather_axis(ny, "y", nsend.at[0], nrecv.at[0])
    nz_out, nz_in = gather_axis(nz, "z", nsend.at[1], nrecv.at[1])

    def fcopy(ts, q):
        return pltpu.make_async_copy(uf.at[ts, q], uf_out.at[ts, q], fsem.at[ts, q])

    weight = w_ref[...].astype(F32)

    def forward(e_s, stage, etb):
        def etcopy(i):
            part = VB // 3
            cols = pl.ds(pl.multiple_of(vstart + i * part, LANE), part)
            return pltpu.make_async_copy(et_ref.at[:, cols], etb.at[:, pl.ds(i * part, part)], etsem.at[i])

        parts = [etcopy(i) for i in range(3)]
        start(parts)
        start([own_ge(half, q) for half in PAIR for q in PAIR])
        ints[0] = ints_ref[...]
        hits[...] = jnp.zeros_like(hits)
        for half in PAIR:
            for q in PAIR:
                rows = h_ref[:, pl.ds(half * TS + q * TB, TB)].astype(F32)
                inv = lax.rsqrt(jnp.mean(rows * rows, axis=0, keepdims=True) + RMS_EPS)
                uf[half, q] = rows * inv
        wait([own_ge(half, q) for half in PAIR for q in PAIR])
        for q in PAIR:
            gst[q] = gb[core, q].astype(F32)
        start([keep_ge(q) for q in PAIR])

        def ebody(i, _):
            lanes = pl.ds(pl.multiple_of(i * EC, EC), EC)
            e_s[lanes, :] = etb[:, lanes].T
            return 0

        for i, part in enumerate(parts):
            part.wait()
            lax.fori_loop(4 * i, 4 * i + 4, ebody, 0)
        wait([keep_ge(q) for q in PAIR])
        pl.semaphore_wait(barrier, len(peers))
        start(own[:2])
        start([icopy(d) for d in HOPS])
        start(own[2:])
        iota = lax.broadcasted_iota(I32, (SUB, TB), 0)

        def ocopy(ts, q, slot):
            return pltpu.make_async_copy(stage.at[slot], logit_ref.at[ts, :, pl.ds(pl.multiple_of(q * TB, TB), TB)], osem.at[slot])

        def zt_step(s, _):
            j = four(s)
            r = jnp.where(s < 4, 0, jnp.where(s < 12, 1 + two(j), 3))
            q = jnp.where((s < 8) | (s >= 12), two(j), 1 - two(j))
            half = jnp.where(s < 4, j // 2, jnp.where(j < 2, core, other))
            ts = 2 * r + half

            @pl.when(s == 4)
            def _():
                for i, (r, q) in enumerate(FIRST):
                    own[i].wait_recv()
                    onward[i].start()
                    pcopy(r, q).start()
                arrive([icopy(d) for d in HOPS])
                start(stat_copies(0))
                start(gmine[:2])

            @pl.when(s == 6)
            def _():
                arrive([parrive(r, q) for r, q in FIRST])

            @pl.when(s == 8)
            def _():
                for i, (r, q) in enumerate(LATER):
                    own[2 + i].wait_recv()
                    pcopy(r, q).start()
                count = jnp.sum(ints[:, :, :, 2, :].astype(F32))
                ny[yi] = jnp.full((SUB, LANE), count, F32)
                start(ny_out)

            @pl.when(s == 10)
            def _():
                arrive([parrive(r, q) for r, q in LATER])
                arrive(ny_in)
                nz[zi] = sum4(ny)
                start(nz_out)

            @pl.when(s == 12)
            def _():
                for i in PAIR:
                    onward[i].wait_recv()
                    pcopy(3, i).start()
                start(stat_copies(1) + stat_copies(2))

            @pl.when(s == 14)
            def _():
                arrive([parrive(3, i) for i in PAIR])

            slot = two(s)

            @pl.when(s >= 2)
            def _():
                ocopy(ts, q, slot).wait()

            zt = (uf[ts, q] * weight).astype(BF16)
            zb[ts, q] = zt
            fcopy(ts, q).start()
            tgt = ints[r, half, q, ROW0, :] - vstart
            m8 = jnp.full((SUB, TB), -jnp.inf, F32)
            s8 = jnp.zeros((SUB, TB), F32)
            t8 = jnp.zeros((SUB, TB), F32)
            for vc in range(VB // CH):
                l = jnp.dot(e_s[span(vc, CH), :], zt, preferred_element_type=F32)
                stage[slot, span(vc, CH), :] = l
                mn = m8
                for i in range(CH // SUB):
                    mn = jnp.maximum(mn, l[span(i, SUB)])
                s8 = s8 * jnp.exp(m8 - mn)
                m8 = mn
                for i in range(CH // SUB):
                    li = l[span(i, SUB)]
                    s8 = s8 + jnp.exp(li - mn)
                    t8 = t8 + jnp.where(iota == tgt - (vc * CH + i * SUB), li, 0.0)
            m = jnp.max(m8, axis=0, keepdims=True)
            at_row = 4 * half + 2 * q
            stats[0, r, pl.ds(at_row, 1), :] = m
            stats[0, r, pl.ds(at_row + 1, 1), :] = jnp.sum(s8 * jnp.exp(m8 - m), axis=0, keepdims=True)
            hits[...] += jnp.sum(t8, axis=0, keepdims=True) * ints[r, half, q, ROW2, :].astype(F32)
            ocopy(ts, q, slot).start()
            return 0

        lax.fori_loop(0, NS * 2, zt_step, 0)
        sent(own + onward + [pcopy(r, q) for r in HOPS for q in PAIR])
        wait([fcopy(ts, q) for ts in range(NS) for q in PAIR])
        start(stat_copies(3))
        start(gmine[2:])
        wait([ocopy(0, 0, slot) for slot in PAIR])

    pl.run_scoped(forward, V((VB, D), BF16), V((2, VB, TB), F32), V((D, VB), BF16))

    def backward(dz, de, lbuf, et_s):
        iota = lax.broadcasted_iota(I32, (V2, TS), 0)

        def near_load(vc):
            slot, rows = two(vc), pl.ds(pl.multiple_of(vc * V2, V2), V2)
            cols = pl.ds(pl.multiple_of(vstart + vc * V2, LANE), V2)
            return [
                pltpu.make_async_copy(logit_ref.at[pl.ds(0, NS - 2), rows, :], lbuf.at[slot, pl.ds(0, NS - 2)], lsem.at[slot, 0]),
                pltpu.make_async_copy(et_ref.at[:, cols], et_s.at[slot, :, pl.ds(0, V2)], esem.at[slot]),
            ]

        def far_load(u):
            slot, far = two(u), pl.ds(NS - 2, 2)
            cols = pl.ds(pl.multiple_of(vstart + u * EC, LANE), EC)
            return [
                pltpu.make_async_copy(logit_ref.at[far, pl.ds(pl.multiple_of(u * EC + k * V2, V2), V2), :], lbuf.at[slot, pl.ds(2 * k, 2)], lsem.at[slot, k])
                for k in PAIR
            ] + [pltpu.make_async_copy(et_ref.at[:, cols], et_s.at[slot], esem.at[slot])]

        for slot in PAIR:
            start(far_load(slot))
        dz[...] = jnp.zeros_like(dz)
        arrive(nz_in)
        total = sum4(nz)[ROW0, ROW0]
        for r in QUAD:
            arrive(stat_copies(r))
        loss = -hits[...]
        for r in QUAD:
            for half in PAIR:
                for q in PAIR:
                    lanes = span(q, TB)
                    top, low = (span(4 * half + 2 * q + i, 1) for i in PAIR)
                    ms = [stats[i, r, top, :] for i in range(NS)]
                    m = functools.reduce(jnp.maximum, ms)
                    tot = sum(stats[i, r, low, :] * jnp.exp(ms[i] - m) for i in range(NS))
                    lse = m + jnp.log(tot)
                    mask = ints[r, half, q, ROW2, :].astype(F32)
                    row[2 * r + half, ROW0, lanes] = lse
                    row[2 * r + half, ROW1, lanes] = mask / total
                    ids[2 * r + half, ROW0, lanes] = ints[r, half, q, ROW0, :] - vstart
                    ids[2 * r + half, ROW1, lanes] = ints[r, half, q, ROW1, :] - vstart
                    if r == 0:
                        loss = loss + jnp.where(core == half, mask * lse, 0.0)
        aux[0, ROW1, :] = jnp.broadcast_to(jnp.sum(loss, axis=1, keepdims=True), (1, TB))
        aux[1, ROW1, :] = jnp.broadcast_to(total, (1, TB))

        def piece(p):
            third = p >= 8
            hi = two(p // 2)
            r = jnp.where(third, 3, 1 + hi)
            q = jnp.where(third, hi, jnp.where(p < 4, hi, 1 - hi))
            return 2 * r + two(p), q

        def stage_in(p):
            ts, q = piece(p)
            return pltpu.make_async_copy(gall.at[ts, q], gst.at[two(p)], gsem.at[two(p)])

        def convert(p):
            ts, q = piece(p)
            stage_in(p).wait()
            gb[ts, q] = gst[two(p)].astype(BF16)

        def de_index(u, zblk, qtr):
            return jnp.where(two(u) == 0, zblk * 4 + qtr, qtr * 4 + zblk)

        def dlogits(tile, ts, base):
            p = jnp.exp(tile - row[ts, ROW0, :])
            return (jnp.where(iota == ids[ts, ROW0, :] - base, p - 1.0, p) * row[ts, ROW1, :]).astype(BF16)

        def products(et, ds, ts, accs):
            part = sum(jnp.dot(et[:, span(k, V2)], d, preferred_element_type=F32) for k, d in enumerate(ds))
            for q in PAIR:
                dz[ts % 2, ts // 2, q] += part[:, span(q, TB)]
                for k, d in enumerate(ds):
                    a = lax.dot_general(zb[ts, q], d[:, span(q, TB)], NT, preferred_element_type=F32)
                    accs[k] = a if accs[k] is None else accs[k] + a

        def far_step(u):
            slot, accs = two(u), [None, None]
            wait(far_load(u))
            et = et_s[slot]
            for half in PAIR:
                ts = NS - 2 + half
                products(et, [dlogits(lbuf[slot, 2 * k + half], ts, u * EC + k * V2) for k in PAIR], ts, accs)
            for zblk in QUAD:
                for qtr in QUAD:
                    de[u, de_index(u, zblk, qtr)] = accs[qtr // 2][span(zblk, ROWS), span(qtr % 2, LANE)]

            @pl.when(u + 2 < 2 * NP)
            def _():
                start(far_load(u + 2))

            @pl.when(u + 2 >= 2 * NP)
            def _():
                start(near_load(u + 2 - 2 * NP))

        def near_step(vc):
            slot, accs, u = two(vc), [None], vc // 2
            wait(near_load(vc))
            et = et_s[slot, :, span(0, V2)]
            for ts in range(NS - 2):
                products(et, [dlogits(lbuf[slot, ts], ts, vc * V2)], ts, accs)
            for zblk in QUAD:
                for ql in PAIR:
                    de[u, de_index(u, zblk, slot * 2 + ql)] += accs[0][span(zblk, ROWS), span(ql, LANE)]

            @pl.when(vc + 2 < N2)
            def _():
                start(near_load(vc + 2))

        def lookup_step(vc):
            base = vc * V2
            acc = None
            for ts in range(NS):
                o = jnp.where(iota == ids[ts, ROW1, :] - base, 1.0, 0.0).astype(BF16)
                for q in PAIR:
                    a = lax.dot_general(gb[ts, q], o[:, span(q, TB)], NT, preferred_element_type=F32)
                    acc = a if acc is None else acc + a
            u = vc // 2
            for zblk in QUAD:
                for ql in PAIR:
                    de[u, de_index(u, zblk, two(vc) * 2 + ql)] += acc[span(zblk, ROWS), span(ql, LANE)]

        def lookups(first):
            def one(i, _):
                lookup_step(first + i)
                return 0

            lax.fori_loop(0, 4, one, 0)

        def a1(p, c):
            a, _ = AXES[c]
            k, op = two(p), at(a, 2) * 4
            return [remote(de.at[2 * p + c, pl.ds(op + 2 * i, 2)], ra1.at[c, k, i], a1s.at[c, k, i], a1r.at[c, k, i], hop(a, i)) for i in PAIR]

        def a2(p, c):
            a, _ = AXES[c]
            k = two(p)
            return [remote(de.at[2 * p + c, pl.ds(at(a, side(i)) * 4, 4)], ra2.at[c, k, i], a2s.at[c, k, i], a2r.at[c, k, i], hop(a, i)) for i in PAIR]

        def b1(p, c):
            a, b = AXES[c]
            k, i2 = two(p), me[a] * 4 + at(b, 2)
            return [remote(de.at[2 * p + c, i2, pl.ds(HROWS * i, HROWS)], rb1.at[c, k, i], b1s.at[c, k, i], b1r.at[c, k, i], hop(b, i)) for i in PAIR]

        def b2(p, c):
            a, b = AXES[c]
            k = two(p)
            return [remote(de.at[2 * p + c, me[a] * 4 + at(b, side(i))], rb2.at[c, k, i], b2s.at[c, k, i], b2r.at[c, k, i], hop(b, i)) for i in PAIR]

        def do_a1(p):
            for c in PAIR:
                start(a1(p, c))

        def do_a2(p):
            k = two(p)
            for c in PAIR:
                a, _ = AXES[c]
                wait(a1(p, c))
                for i in PAIR:
                    for j in PAIR:
                        de[2 * p + c, at(a, side(i)) * 4 + 2 * i + j] += ra1[c, k, i, j]
                start(a2(p, c))

        def do_b1(p):
            k = two(p)
            for c in PAIR:
                a, _ = AXES[c]
                wait(a2(p, c))
                for j in QUAD:
                    de[2 * p + c, me[a] * 4 + j] += ra2[c, k, 0, j] + ra2[c, k, 1, j]
                start(b1(p, c))

        def do_b2(p):
            k = two(p)
            for c in PAIR:
                a, b = AXES[c]
                wait(b1(p, c))
                for i in PAIR:
                    de[2 * p + c, me[a] * 4 + at(b, side(i)), span(i, HROWS)] += rb1[c, k, i]
                start(b2(p, c))

        def do_f(p):
            k = two(p)
            for c in PAIR:
                a, b = AXES[c]
                wait(b2(p, c))
                de[2 * p + c, me[a] * 4 + me[b]] += rb2[c, k, 0] + rb2[c, k, 1]

        def col(b, dy, dx):
            dst = at("y", dy) * 4 + at("x", dx)
            return remote(sb.at[b, dst], rv.at[b, yi * 4 + xi], ass.at[b, dy * 4 + dx], asr.at[b, dy * 4 + dx], {"y": at("y", dy), "x": at("x", dx)})

        def col_arrive(b, dy, dx):
            src = at("y", -dy % 4) * 4 + at("x", -dx % 4)
            return remote(sb.at[b, src], rv.at[b, src], ass.at[b, dy * 4 + dx], asr.at[b, dy * 4 + dx], {"y": at("y", dy), "x": at("x", dx)})

        def do_cols(b):
            for k in range(NP):
                first, second = AXES[k % 2]
                mine = me[first] * 4 + me[second]
                for s in range(16):
                    sb[b, s, span(k, OWN), :] = de[NP * b + k, mine, span(s, OWN), :]
            start([col(b, dy, dx) for dy, dx in FAR])
            rv[b, yi * 4 + xi] = sb[b, yi * 4 + xi]

        def do_assemble(b):
            arrive([col_arrive(b, dy, dx) for dy, dx in FAR])
            for s in range(16):
                for k in range(NP):
                    lane = (s % 4) * VB + (NP * b + k) * EC + (s // 4) * LANE
                    de_out[:, pl.ds(lane, LANE)] = rv[b, s, span(k, OWN), :]

        def dcopy(r):
            return remote(dz.at[other, r], uf.at[r], dps.at[r], dpr.at[r], {"tp": other})

        def unit_in(r, q):
            return pltpu.make_async_copy(uf_out.at[2 * r + core, q], gst.at[q], gsem.at[q])

        def fetch(r):
            start([unit_in(r, q) for q in PAIR])

        def core_sum(r):
            dcopy(r).wait_recv()
            for q in PAIR:
                dz[core, r, q] += uf[r, q]

        def gain_sum(r, dg):
            wait([unit_in(r, q) for q in PAIR])
            for q in PAIR:
                for j in PAIR:
                    dg = dg + dz[core, r, q, :, span(j, LANE)] * gst[q, :, span(j, LANE)]
            return dg

        def c1(i, q):
            return remote(dz.at[core, 3, q, pl.ds(HD * i, HD)], uf.at[6, i, pl.ds(HD * q, HD)], c1s.at[i, q], c1r.at[i, q], hop("x", i))

        def c2(i):
            return remote(dz.at[core, 2 - i], uf.at[4 + i], c2s.at[i], c2r.at[i], hop("x", i))

        def far_unit(u, _):
            @pl.when(u == 2)
            def _():
                for i, (r, q) in enumerate(FIRST):
                    gmine[i].wait_recv()
                    gonward[i].start()
                    gpcopy(r, q).start()

            @pl.when(u == 4)
            def _():
                arrive([gparrive(r, q) for r, q in FIRST])
                stage_in(0).start()

            @pl.when((u >= 5) & (u < 9))
            def _():
                convert(u - 5)

            @pl.when((u >= 5) & (u < 8))
            def _():
                stage_in(u - 4).start()

            far_step(u)
            return 0

        lax.fori_loop(0, 2 * NP, far_unit, 0)
        dcopy(3).start()

        def near_chunk(vc, _):
            @pl.when(vc == 1)
            def _():
                for i, (r, q) in enumerate(LATER):
                    gmine[2 + i].wait_recv()
                    gpcopy(r, q).start()

            @pl.when(vc == 2)
            def _():
                arrive([gparrive(r, q) for r, q in LATER])
                stage_in(4).start()
                core_sum(3)
                start([c1(i, q) for i in PAIR for q in PAIR])

            @pl.when((vc >= 3) & (vc < 7))
            def _():
                convert(vc + 1)

            @pl.when((vc >= 3) & (vc < 6))
            def _():
                stage_in(vc + 2).start()

            near_step(vc)
            return 0

        lax.fori_loop(0, NA, near_chunk, 0)
        for i in PAIR:
            gonward[i].wait_recv()
            gpcopy(3, i).start()
        arrive([gparrive(3, i) for i in PAIR])
        stage_in(8).start()
        for p in range(8, 12):
            if p < 11:
                stage_in(p + 1).start()
            convert(p)

        def phase_c(p, _):
            @pl.when(p >= 1)
            def _():
                do_a2(p - 1)

            lookups(4 * p)

            @pl.when(p >= 2)
            def _():
                do_b2(p - 2)

            do_a1(p)

            def more(i, _):
                near_step(NA + 3 * p + i)
                return 0

            lax.fori_loop(0, 3, more, 0)

            @pl.when(p >= 2)
            def _():
                do_f(p - 2)

            @pl.when(p >= 1)
            def _():
                do_b1(p - 1)

            return 0

        lax.fori_loop(0, NP - 1, phase_c, 0)

        start([dcopy(r) for r in (1, 2, 0)])
        fetch(3)
        do_a2(4)
        do_cols(0)
        dg = gain_sum(3, jnp.zeros((D, LANE), F32))
        fetch(1)
        for i in (1, 0):
            core_sum(2 - i)
            dg = gain_sum(2 - i, dg)
            fetch(2 * i)
            for q in PAIR:
                c1(i, q).wait()
                dz[core, 2 - i, q, span(i, HD)] += uf[6, i, span(q, HD)]
            c2(i).start()
        lookups(20)
        do_b2(3)
        do_a1(5)
        core_sum(0)
        dg = gain_sum(0, dg)
        st[core] = jnp.zeros((SUB, 640), F32)
        st[core, ROW0, span(0, D)] = jnp.sum(dg.T, axis=0, keepdims=True)
        st[core, ROW1, span(0, TB)] = aux[0, ROW1, :]
        pair_copy = remote(st.at[core], st.at[core], sts, str_, {"tp": other})
        pair_arrive = remote(st.at[core], st.at[other], sts, str_, {"tp": other})
        pair_copy.start()
        do_b1(4)
        pair_arrive.wait()
        sz[zi] = st[0] + st[1]
        sums = [gather_axis(buf, axis, sas.at[k], sar.at[k]) for k, (buf, axis) in enumerate(((sz, "z"), (sy, "y"), (sx, "x")))]
        start(sums[0][0])
        do_a2(5)
        do_f(3)
        do_b2(4)
        wait(sums[0][1])
        sy[yi] = sum4(sz)
        start(sums[1][0])
        do_f(4)
        do_b1(5)
        wait(sums[1][1])
        sx[xi] = sum4(sy)
        start(sums[2][0])
        do_b2(5)
        do_f(5)
        do_cols(1)

        for q in PAIR:
            rows = h_ref[:, pl.ds(pl.multiple_of(core * TS + q * TB, TB), TB)].astype(F32)
            inv = lax.rsqrt(jnp.mean(rows * rows, axis=0, keepdims=True) + RMS_EPS)
            gst[q] = rows * inv
            aux[q, ROW0, :] = inv
        wait([c2(i) for i in PAIR])
        for q in PAIR:
            unit, inv = gst[q], aux[q, ROW0, :]
            gu = (dz[core, 0, q] + uf[4, q] + uf[5, q]) * weight
            dz[core, 3, q] = inv * (gu - unit * jnp.mean(gu * unit, axis=0, keepdims=True))
        half_copy = remote(dz.at[core, 3], uf.at[7], hs, hr, {"tp": other})
        half_copy.start()
        do_assemble(0)
        do_assemble(1)
        wait(sums[2][1])
        sum_out[...] = sum4(sx)
        sum_out[ROW1, span(0, TB)] = sum_out[ROW1, span(0, TB)] / aux[1, ROW1, :]
        half_copy.wait()
        for half in PAIR:
            for q in PAIR:
                gb[half, q] = jnp.where(core == half, dz[core, 3, q], uf[7, q]).astype(BF16)
                out_dh(half, q).start()
        wait([out_dh(half, q) for half in PAIR for q in PAIR])

        sent(gmine + gonward + [gpcopy(r, q) for r in HOPS for q in PAIR] + [dcopy(r) for r in QUAD])
        sent([col(b, dy, dx) for b in PAIR for dy, dx in FAR])
    pl.run_scoped(
        backward, V((2, GX, 2, D, TB), F32), V((2 * NP, 16, ROWS, LANE), F32), V((2, NS, V2, TS), F32), V((2, D, EC), BF16)
    )
    sent([icopy(d) for d in HOPS] + ny_out + nz_out)
    for r in QUAD:
        sent(stat_copies(r))


def call(h_t, ge_t, w, ints, et):
    links = [DMA((2, 2, 2))] * 8
    return pl.pallas_call(
        kernel,
        out_shape=(
            SDS((OWN, VL), F32), SDS((D, TOK), BF16), SDS(SUMS, F32),
            SDS((NS, VB, TS), F32), SDS(TOKENS, F32), SDS(TOKENS, F32),
        ),
        in_specs=[VMEM, ANY, VMEM, VMEM, ANY],
        out_specs=(VMEM, ANY, VMEM) + (ANY,) * 3,
        scratch_shapes=[
            V(TOKENS, F32),
            *[V(TOKENS, BF16)] * 2,
            V((2, D, TB), F32),
            V((GX, 2, 2, SUB, TB), I32),
            V((NS, GX, SUB, TB), F32), V((1, TB), F32),
            *[V((GX, SUB, LANE), F32)] * 2,
            V((NS, 2, TS), F32), V((NS, 2, TS), I32), V((2, SUB, TB), F32),
            V((2, 2, 2, 2, ROWS, LANE), F32),
            V((2, 2, 2, GX, ROWS, LANE), F32),
            V((2, 2, 2, HROWS, LANE), F32),
            V((2, 2, 2, ROWS, LANE), F32),
            *[V((2, 16, 56, LANE), F32)] * 2,
            V((2, *SUMS), F32), *[V((GX, *SUMS), F32)] * 3,
            DMA((3,)), DMA((2,)), DMA((2, 2)), *[DMA((2,))] * 2, DMA((2, 2)), *[DMA((NS, 2))] * 2,
            DMA((NS,)), *[DMA((GX, 2))] * 3, *[DMA((GX,))] * 2, *[DMA((NS, GX))] * 2, *[DMA((2, GX))] * 2,
            DMA((NS,)), *[DMA((GX, 2))] * 3, *links,
            *[DMA((2, 16))] * 2, *[DMA((GX,))] * 2, *[DMA((2, 2))] * 2, *[DMA((2,))] * 2, *[DMA(())] * 4, *[DMA((3, GX))] * 2,
        ],
        compiler_params=pltpu.CompilerParams(vmem_limit_bytes=67043328, collective_id=0, has_side_effects=True),
    )(h_t, ge_t, w, ints, et)


def solution(mesh):
    mesh4 = Mesh(mesh.devices.reshape(2, 4, 4, 4), ("tp", "z", "y", "x"))

    def local_step(hidden, norm_w, embed, targets, loss_mask, token_ids, grad_embed):
        base = lax.axis_index("tp") * VL
        h_t = hidden.reshape(TOK, D).T
        ge_t = grad_embed.reshape(TOK, D).T
        own = [a.reshape(2, 2, 1, TB) for a in (targets - base, token_ids - base, loss_mask)]
        ints = jnp.concatenate(own + own[:1] * 5, axis=2)
        de, dh, sums, *_ = call(h_t, ge_t, norm_w.reshape(D, 1), ints, embed.T)
        return sums[1, 0], dh.T.reshape(1, TOK, D), sums[0, :D], de.T

    dp = ("z", "y", "x")
    return jax.shard_map(
        local_step,
        mesh=mesh4,
        in_specs=(P(dp), P(), P("tp"), P(dp), P(dp), P(dp), P(dp)),
        out_specs=(P(), P(dp), P(), P("tp", dp)),
        check_vma=False,
    )
```

time: 1150 us -> 244 us (0.21)
  blocking collectives: 341 us -> 0 us
  waiting for transfers between devices: 315 us -> 0 us
  Pallas kernels: 0 us -> 230 us
  other arithmetic: 226 us -> 0.71 us
  matrix products: 155 us -> 0 us
  local copies, waits for them, and re-layouts: 86.6 us -> 8.98 us
  between operations: 17.4 us -> 0.66 us
    psum x3 -> x0, blocking collectives: 338 us -> none  [the longest x1 153 us: local_step(): lax.psum(jnp.sum(mask_rows * (log_norm - target_logit)), 'dp') / token_count]
    unnamed x3 -> x0, waiting for transfers between devices: 315 us -> none
    pallas_call x0 -> x1, Pallas kernels: none -> 230 us  [call(): pl.pallas_call(kernel, out_shape=(SDS((OWN, VL), F32), SDS((D, TOK), BF16...]
    dot_general x3 -> x0, matrix products: 155 us -> none  [the longest x1 64.5 us: local_step(): jnp.einsum('tv,td->vd', dlogits, z_rows, preferred_element_type=jnp.float32)]
    scatter-add x1 -> x0, other arithmetic: 128 us -> none  [local_step(): jax.ops.segment_sum(grad_embed.reshape(tokens, d_model).astype(jnp.float3...]
    scatter-add x1 -> x0, local copies, waits for them, and re-layouts: 58.7 us -> none  [local_step(): jax.ops.segment_sum(grad_embed.reshape(tokens, d_model).astype(jnp.float3...]
    convert_element_type x3 -> x0, other arithmetic: 51.7 us -> none  [the longest x1 49.3 us: local_step(): (jnp.where(is_target, soft_probs - 1.0, soft_probs) * (mask_rows / token_...]
    reduce_sum x5 -> x0, other arithmetic: 41.9 us -> none  [the longest x1 36.6 us: local_step(): sum_exp = lax.psum(jnp.sum(shifted, axis=-1, keepdims=True), 'tp')]
  transfers between devices with their start and end apart: 2 -> 0, of which waited for: 1 -> 0; matrix products, arithmetic and copies ran while one was open for 25% -> 0% of each run, Pallas kernels for 0% -> 0%
where the time goes in v4:
time: 244 us; the launch traced here: 240 us
  Pallas kernels  230 us (94%)
  local copies, waits for them, and re-layouts  8.98 us (4%)
    pallas_call x1, Pallas kernels, call(): pl.pallas_call(kernel, out_shape=(SDS((OWN, VL), F32), SDS((D, TOK), BF16...  230 us

profile of v4, /device:TPU:1, one launch (start us, length us, event | category | flops | bytes accessed | tf_op | source)
XLA Modules:
  0.0 240.5 jit_solution(4169262847075635663)
XLA Ops:
  0.6 0.7 broadcast_subtract_fusion
  1.3 1.4 concatenate.3.ints_ref
  2.7 1.5 reshape.36.w_ref
  4.2 230.1 %shard_map.102 = (f32[9,24576]{1,0:T(8,128)}, bf16[576,1024]{1,0:T(8,128)(2,1)}, f32[8,640]{1,0:T(8,128)}, f32[8,6144,512]{2,1,0:T(8,128)}, f32[8,2,576,256]{3,2,1,0:T(8,128)}, /*index=5*/f32[8,2,576,256]{3,2,1,0:T(8,128)}) custom-call(bf16[576,1024]{1,0:T(8,128)(2,1)} %bitcast.17, bf16[576,1024]{1,0:T(8,128)(2,1)} %bitcast.18, ...), custom_call_target="tpu_custom_call" | custom-call | tf_op jit(solution)/shard_map/pallas_call | solution.py:723
  234.3 0.0 copy-start
  234.3 1.3 slice.6
  235.6 1.3 slice_reduce_fusion
  236.9 2.4 copy.14
  239.3 0.0 copy-done
  239.3 1.1 copy.15
Async XLA Ops:
  234.3 5.0 %copy-start = (f32[9,24576]{1,0:T(8,128)S(1)}, f32[9,24576]{1,0:T(8,128)}, u32[]{:S(2)}) copy-start(f32[9,24576]{1,0:T(8,128)} %get-tuple-element.9) | copy-start | bytes 2654212

commit v5 on v4

--- a/solution.py
+++ b/solution.py
@@ -28,7 +28,7 @@
 V, DMA, SDS = pltpu.VMEM, pltpu.SemaphoreType.DMA, jax.ShapeDtypeStruct
 SUB = 8
 TOKENS = (NS, 2, D, TB)
-SUMS = (SUB, 640)
+SUMS = (2, 640)
 GRID = [(dy, dx) for dy in range(4) for dx in range(4)]
 FAR = GRID[1:]
 GROUP = [(d, cross) for d in range(4) for cross in range(2) if d or cross]
@@ -65,17 +65,18 @@
     return pltpu.make_async_remote_copy(src_ref=src, dst_ref=dst, send_sem=send, recv_sem=recv, device_id=where, device_id_type=MESH)
 
 
+NEARS, BATCHES = NS - 2, range(3)
 NP = 6
-NA = 9
+NA = 4
 AXES = ("zy", "yz")
 
 
 def kernel(
-    h_ref, ge_ref, w_ref, ints_ref, et_ref,
+    h_ref, ge_ref, w_ref, tgt_ref, mask_ref, tok_ref, et_ref,
     de_out, dh_out, sum_out, logit_ref, uf_out, gall,
     uf, zb, gb, gst, ints, stats, hits, ny, nz, row, ids, aux,
-    ra1, ra2, rb1, rb2, sb, rv, st, sx, sy, sz,
-    etsem, osem, lsem, esem, gsem, gown, zsem, fsem,
+    gain, de_s, ra1, ra2, rb1, rb2, sb, rv, st, sx, sy, sz,
+    desem, etsem, osem, lsem, esem, gsem, gown, zsem, fsem,
     usend, urecv, psend, precv, isend, irecv, ssend, srecv, nsend, nrecv,
     gsend, grecv, gpsend, gprecv, a1s, a1r, a2s, a2r, b1s, b1r, b2s, b2r,
     ass, asr, dps, dpr, c1s, c1r, c2s, c2r, hs, hr, sts, str_, sas, sar,
@@ -178,14 +179,18 @@
 
     def forward(e_s, stage, etb):
         def etcopy(i):
-            part = VB // 3
-            cols = pl.ds(pl.multiple_of(vstart + i * part, LANE), part)
-            return pltpu.make_async_copy(et_ref.at[:, cols], etb.at[:, pl.ds(i * part, part)], etsem.at[i])
-
-        parts = [etcopy(i) for i in range(3)]
-        start(parts)
+            cols = pl.ds(pl.multiple_of(vstart + i * EC, LANE), EC)
+            return pltpu.make_async_copy(et_ref.at[:, cols], etb.at[:, pl.ds(pl.multiple_of(i * EC, EC), EC)], etsem.at[i])
+
+        start([etcopy(i) for i in range(2 * NP)])
         start([own_ge(half, q) for half in PAIR for q in PAIR])
-        ints[0] = ints_ref[...]
+        ints[0] = jnp.zeros_like(ints[0])
+        for half in PAIR:
+            for q in PAIR:
+                lanes = span(2 * half + q, TB)
+                ints[0, half, q, ROW0, :] = tgt_ref[:, lanes] - core * VL
+                ints[0, half, q, ROW1, :] = tok_ref[:, lanes] - core * VL
+                ints[0, half, q, ROW2, :] = mask_ref[:, lanes]
         hits[...] = jnp.zeros_like(hits)
         for half in PAIR:
             for q in PAIR:
@@ -198,13 +203,12 @@
         start([keep_ge(q) for q in PAIR])
 
         def ebody(i, _):
+            etcopy(i).wait()
             lanes = pl.ds(pl.multiple_of(i * EC, EC), EC)
             e_s[lanes, :] = etb[:, lanes].T
             return 0
 
-        for i, part in enumerate(parts):
-            part.wait()
-            lax.fori_loop(4 * i, 4 * i + 4, ebody, 0)
+        lax.fori_loop(0, 2 * NP, ebody, 0)
         wait([keep_ge(q) for q in PAIR])
         pl.semaphore_wait(barrier, len(peers))
         start(own[:2])
@@ -312,12 +316,12 @@
             slot, rows = two(vc), pl.ds(pl.multiple_of(vc * V2, V2), V2)
             cols = pl.ds(pl.multiple_of(vstart + vc * V2, LANE), V2)
             return [
-                pltpu.make_async_copy(logit_ref.at[pl.ds(0, NS - 2), rows, :], lbuf.at[slot, pl.ds(0, NS - 2)], lsem.at[slot, 0]),
+                pltpu.make_async_copy(logit_ref.at[pl.ds(0, NEARS), rows, :], lbuf.at[slot, pl.ds(0, NEARS)], lsem.at[slot, 0]),
                 pltpu.make_async_copy(et_ref.at[:, cols], et_s.at[slot, :, pl.ds(0, V2)], esem.at[slot]),
             ]
 
-        def far_load(u):
-            slot, far = two(u), pl.ds(NS - 2, 2)
+        def far_load(u, ts=NEARS):
+            slot, far = two(u), pl.ds(ts, 2)
             cols = pl.ds(pl.multiple_of(vstart + u * EC, LANE), EC)
             return [
                 pltpu.make_async_copy(logit_ref.at[far, pl.ds(pl.multiple_of(u * EC + k * V2, V2), V2), :], lbuf.at[slot, pl.ds(2 * k, 2)], lsem.at[slot, k])
@@ -374,10 +378,15 @@
             p = jnp.exp(tile - row[ts, ROW0, :])
             return (jnp.where(iota == ids[ts, ROW0, :] - base, p - 1.0, p) * row[ts, ROW1, :]).astype(BF16)
 
-        def products(et, ds, ts, accs):
+        def add_dz(et, ds, ts):
             part = sum(jnp.dot(et[:, span(k, V2)], d, preferred_element_type=F32) for k, d in enumerate(ds))
             for q in PAIR:
                 dz[ts % 2, ts // 2, q] += part[:, span(q, TB)]
+
+        def products(et, ds, ts, accs):
+            if ts >= 2:
+                add_dz(et, ds, ts)
+            for q in PAIR:
                 for k, d in enumerate(ds):
                     a = lax.dot_general(zb[ts, q], d[:, span(q, TB)], NT, preferred_element_type=F32)
                     accs[k] = a if accs[k] is None else accs[k] + a
@@ -387,7 +396,7 @@
             wait(far_load(u))
             et = et_s[slot]
             for half in PAIR:
-                ts = NS - 2 + half
+                ts = NEARS + half
                 products(et, [dlogits(lbuf[slot, 2 * k + half], ts, u * EC + k * V2) for k in PAIR], ts, accs)
             for zblk in QUAD:
                 for qtr in QUAD:
@@ -401,11 +410,21 @@
             def _():
                 start(near_load(u + 2 - 2 * NP))
 
+        def own_step(u):
+            slot = two(u)
+            wait(far_load(u, 0))
+            for half in PAIR:
+                add_dz(et_s[slot], [dlogits(lbuf[slot, 2 * k + half], half, u * EC + k * V2) for k in PAIR], half)
+
+            @pl.when(u + 2 < 2 * NP)
+            def _():
+                start(far_load(u + 2, 0))
+
         def near_step(vc):
             slot, accs, u = two(vc), [None], vc // 2
             wait(near_load(vc))
             et = et_s[slot, :, span(0, V2)]
-            for ts in range(NS - 2):
+            for ts in range(NEARS):
                 products(et, [dlogits(lbuf[slot, ts], ts, vc * V2)], ts, accs)
             for zblk in QUAD:
                 for ql in PAIR:
@@ -435,25 +454,28 @@
 
             lax.fori_loop(0, 4, one, 0)
 
+        def unit(p, c):
+            return 2 * p + c
+
         def a1(p, c):
             a, _ = AXES[c]
             k, op = two(p), at(a, 2) * 4
-            return [remote(de.at[2 * p + c, pl.ds(op + 2 * i, 2)], ra1.at[c, k, i], a1s.at[c, k, i], a1r.at[c, k, i], hop(a, i)) for i in PAIR]
+            return [remote(de.at[unit(p, c), pl.ds(op + 2 * i, 2)], ra1.at[c, k, i], a1s.at[c, k, i], a1r.at[c, k, i], hop(a, i)) for i in PAIR]
 
         def a2(p, c):
             a, _ = AXES[c]
             k = two(p)
-            return [remote(de.at[2 * p + c, pl.ds(at(a, side(i)) * 4, 4)], ra2.at[c, k, i], a2s.at[c, k, i], a2r.at[c, k, i], hop(a, i)) for i in PAIR]
+            return [remote(de.at[unit(p, c), pl.ds(at(a, side(i)) * 4, 4)], ra2.at[c, k, i], a2s.at[c, k, i], a2r.at[c, k, i], hop(a, i)) for i in PAIR]
 
         def b1(p, c):
             a, b = AXES[c]
             k, i2 = two(p), me[a] * 4 + at(b, 2)
-            return [remote(de.at[2 * p + c, i2, pl.ds(HROWS * i, HROWS)], rb1.at[c, k, i], b1s.at[c, k, i], b1r.at[c, k, i], hop(b, i)) for i in PAIR]
+            return [remote(de.at[unit(p, c), i2, pl.ds(HROWS * i, HROWS)], rb1.at[c, k, i], b1s.at[c, k, i], b1r.at[c, k, i], hop(b, i)) for i in PAIR]
 
         def b2(p, c):
             a, b = AXES[c]
             k = two(p)
-            return [remote(de.at[2 * p + c, me[a] * 4 + at(b, side(i))], rb2.at[c, k, i], b2s.at[c, k, i], b2r.at[c, k, i], hop(b, i)) for i in PAIR]
+            return [remote(de.at[unit(p, c), me[a] * 4 + at(b, side(i))], rb2.at[c, k, i], b2s.at[c, k, i], b2r.at[c, k, i], hop(b, i)) for i in PAIR]
 
         def do_a1(p):
             for c in PAIR:
@@ -466,7 +488,7 @@
                 wait(a1(p, c))
                 for i in PAIR:
                     for j in PAIR:
-                        de[2 * p + c, at(a, side(i)) * 4 + 2 * i + j] += ra1[c, k, i, j]
+                        de[unit(p, c), at(a, side(i)) * 4 + 2 * i + j] += ra1[c, k, i, j]
                 start(a2(p, c))
 
         def do_b1(p):
@@ -475,7 +497,7 @@
                 a, _ = AXES[c]
                 wait(a2(p, c))
                 for j in QUAD:
-                    de[2 * p + c, me[a] * 4 + j] += ra2[c, k, 0, j] + ra2[c, k, 1, j]
+                    de[unit(p, c), me[a] * 4 + j] += ra2[c, k, 0, j] + ra2[c, k, 1, j]
                 start(b1(p, c))
 
         def do_b2(p):
@@ -484,7 +506,7 @@
                 a, b = AXES[c]
                 wait(b1(p, c))
                 for i in PAIR:
-                    de[2 * p + c, me[a] * 4 + at(b, side(i)), span(i, HROWS)] += rb1[c, k, i]
+                    de[unit(p, c), me[a] * 4 + at(b, side(i)), span(i, HROWS)] += rb1[c, k, i]
                 start(b2(p, c))
 
         def do_f(p):
@@ -492,7 +514,7 @@
             for c in PAIR:
                 a, b = AXES[c]
                 wait(b2(p, c))
-                de[2 * p + c, me[a] * 4 + me[b]] += rb2[c, k, 0] + rb2[c, k, 1]
+                de[unit(p, c), me[a] * 4 + me[b]] += rb2[c, k, 0] + rb2[c, k, 1]
 
         def col(b, dy, dx):
             dst = at("y", dy) * 4 + at("x", dx)
@@ -502,21 +524,26 @@
             src = at("y", -dy % 4) * 4 + at("x", -dx % 4)
             return remote(sb.at[b, src], rv.at[b, src], ass.at[b, dy * 4 + dx], asr.at[b, dy * 4 + dx], {"y": at("y", dy), "x": at("x", dx)})
 
+        def out_de(b, x):
+            lanes = pl.ds(x * VB + b * 4 * EC, 4 * EC)
+            return pltpu.make_async_copy(de_s.at[:, lanes], de_out.at[:, lanes], desem.at[b, x])
+
         def do_cols(b):
-            for k in range(NP):
+            for k in QUAD:
                 first, second = AXES[k % 2]
                 mine = me[first] * 4 + me[second]
                 for s in range(16):
-                    sb[b, s, span(k, OWN), :] = de[NP * b + k, mine, span(s, OWN), :]
+                    sb[b, s, span(k, OWN), :] = de[4 * b + k, mine, span(s, OWN), :]
             start([col(b, dy, dx) for dy, dx in FAR])
             rv[b, yi * 4 + xi] = sb[b, yi * 4 + xi]
 
         def do_assemble(b):
             arrive([col_arrive(b, dy, dx) for dy, dx in FAR])
             for s in range(16):
-                for k in range(NP):
-                    lane = (s % 4) * VB + (NP * b + k) * EC + (s // 4) * LANE
-                    de_out[:, pl.ds(lane, LANE)] = rv[b, s, span(k, OWN), :]
+                for k in QUAD:
+                    lane = (s % 4) * VB + (4 * b + k) * EC + (s // 4) * LANE
+                    de_s[:, pl.ds(lane, LANE)] = rv[b, s, span(k, OWN), :]
+            start([out_de(b, x) for x in QUAD])
 
         def dcopy(r):
             return remote(dz.at[other, r], uf.at[r], dps.at[r], dpr.at[r], {"tp": other})
@@ -532,12 +559,13 @@
             for q in PAIR:
                 dz[core, r, q] += uf[r, q]
 
-        def gain_sum(r, dg):
+        def gain_sum(r):
             wait([unit_in(r, q) for q in PAIR])
+            dg = gain[...]
             for q in PAIR:
                 for j in PAIR:
                     dg = dg + dz[core, r, q, :, span(j, LANE)] * gst[q, :, span(j, LANE)]
-            return dg
+            gain[...] = dg
 
         def c1(i, q):
             return remote(dz.at[core, 3, q, pl.ds(HD * i, HD)], uf.at[6, i, pl.ds(HD * q, HD)], c1s.at[i, q], c1r.at[i, q], hop("x", i))
@@ -556,57 +584,69 @@
             @pl.when(u == 4)
             def _():
                 arrive([gparrive(r, q) for r, q in FIRST])
-                stage_in(0).start()
-
-            @pl.when((u >= 5) & (u < 9))
-            def _():
-                convert(u - 5)
-
-            @pl.when((u >= 5) & (u < 8))
-            def _():
-                stage_in(u - 4).start()
-
-            far_step(u)
-            return 0
-
-        lax.fori_loop(0, 2 * NP, far_unit, 0)
-        dcopy(3).start()
-
-        def near_chunk(vc, _):
-            @pl.when(vc == 1)
+                start([stage_in(p) for p in PAIR])
+
+            @pl.when(u == 8)
             def _():
                 for i, (r, q) in enumerate(LATER):
                     gmine[2 + i].wait_recv()
                     gpcopy(r, q).start()
 
+            @pl.when(u == 10)
+            def _():
+                arrive([gparrive(r, q) for r, q in LATER])
+                start([stage_in(4 + p) for p in PAIR])
+
+            @pl.when((u >= 5) & (u < 9))
+            def _():
+                convert(u - 5)
+
+            @pl.when((u >= 5) & (u < 7))
+            def _():
+                stage_in(u - 3).start()
+
+            @pl.when(u == 11)
+            def _():
+                convert(4)
+                stage_in(6).start()
+
+            far_step(u)
+            return 0
+
+        lax.fori_loop(0, 2 * NP, far_unit, 0)
+        dcopy(3).start()
+
+        def near_chunk(vc, _):
+            @pl.when(vc == 0)
+            def _():
+                convert(5)
+                stage_in(7).start()
+
+            @pl.when((vc >= 1) & (vc < 3))
+            def _():
+                convert(vc + 5)
+
             @pl.when(vc == 2)
             def _():
-                arrive([gparrive(r, q) for r, q in LATER])
-                stage_in(4).start()
                 core_sum(3)
                 start([c1(i, q) for i in PAIR for q in PAIR])
 
-            @pl.when((vc >= 3) & (vc < 7))
-            def _():
-                convert(vc + 1)
-
-            @pl.when((vc >= 3) & (vc < 6))
-            def _():
-                stage_in(vc + 2).start()
+            @pl.when(vc == 3)
+            def _():
+                for i in PAIR:
+                    gonward[i].wait_recv()
+                    gpcopy(3, i).start()
 
             near_step(vc)
             return 0
 
         lax.fori_loop(0, NA, near_chunk, 0)
-        for i in PAIR:
-            gonward[i].wait_recv()
-            gpcopy(3, i).start()
         arrive([gparrive(3, i) for i in PAIR])
-        stage_in(8).start()
+        start([stage_in(8 + p) for p in PAIR])
         for p in range(8, 12):
-            if p < 11:
-                stage_in(p + 1).start()
             convert(p)
+            if p < 10:
+                stage_in(p + 2).start()
 
         def phase_c(p, _):
             @pl.when(p >= 1)
@@ -621,11 +661,15 @@
 
             do_a1(p)
 
+            @pl.when(p == 4)
+            def _():
+                do_cols(0)
+
             def more(i, _):
-                near_step(NA + 3 * p + i)
+                near_step(NA + 4 * p + i)
                 return 0
 
-            lax.fori_loop(0, 3, more, 0)
+            lax.fori_loop(0, 4, more, 0)
 
             @pl.when(p >= 2)
             def _():
@@ -639,50 +683,92 @@
 
         lax.fori_loop(0, NP - 1, phase_c, 0)
 
-        start([dcopy(r) for r in (1, 2, 0)])
-        fetch(3)
+        start([dcopy(r) for r in (1, 2)])
+        fetch(1)
+        for slot in PAIR:
+            start(far_load(slot, 0))
         do_a2(4)
-        do_cols(0)
-        dg = gain_sum(3, jnp.zeros((D, LANE), F32))
-        fetch(1)
-        for i in (1, 0):
+        gain[...] = jnp.zeros_like(gain)
+
+        def to_neighbour(i):
             core_sum(2 - i)
-            dg = gain_sum(2 - i, dg)
-            fetch(2 * i)
             for q in PAIR:
                 c1(i, q).wait()
                 dz[core, 2 - i, q, span(i, HD)] += uf[6, i, span(q, HD)]
             c2(i).start()
-        lookups(20)
+
+        def last_lookups(i, _):
+            lookup_step(20 + i)
+
+            @pl.when(i == 0)
+            def _():
+                to_neighbour(1)
+
+            @pl.when(i == 1)
+            def _():
+                to_neighbour(0)
+
+            @pl.when(i == 2)
+            def _():
+                gain_sum(1)
+                fetch(2)
+
+            return 0
+
+        lax.fori_loop(0, 4, last_lookups, 0)
         do_b2(3)
         do_a1(5)
+
+        def own_unit(u, _):
+            @pl.when(u == 1)
+            def _():
+                do_b1(4)
+
+            @pl.when(u == 2)
+            def _():
+                gain_sum(2)
+                fetch(0)
+
+            @pl.when(u == 5)
+            def _():
+                do_b2(4)
+                do_a2(5)
+
+            @pl.when(u == 8)
+            def _():
+                do_f(3)
+                do_cols(1)
+
+            own_step(u)
+            return 0
+
+        lax.fori_loop(0, 2 * NP, own_unit, 0)
+        dcopy(0).start()
+        do_f(4)
         core_sum(0)
-        dg = gain_sum(0, dg)
-        st[core] = jnp.zeros((SUB, 640), F32)
-        st[core, ROW0, span(0, D)] = jnp.sum(dg.T, axis=0, keepdims=True)
+        gain_sum(0)
+        st[core] = jnp.zeros(SUMS, F32)
+        st[core, ROW0, span(0, D)] = jnp.sum(gain[...].T, axis=0, keepdims=True)
         st[core, ROW1, span(0, TB)] = aux[0, ROW1, :]
         pair_copy = remote(st.at[core], st.at[core], sts, str_, {"tp": other})
         pair_arrive = remote(st.at[core], st.at[other], sts, str_, {"tp": other})
         pair_copy.start()
-        do_b1(4)
+        sums = [gather_axis(buf, axis, sas.at[k], sar.at[k]) for k, (buf, axis) in enumerate(((sz, "z"), (sy, "y"), (sx, "x")))]
+        do_b1(5)
         pair_arrive.wait()
         sz[zi] = st[0] + st[1]
-        sums = [gather_axis(buf, axis, sas.at[k], sar.at[k]) for k, (buf, axis) in enumerate(((sz, "z"), (sy, "y"), (sx, "x")))]
         start(sums[0][0])
-        do_a2(5)
-        do_f(3)
-        do_b2(4)
+        do_assemble(0)
+        do_b2(5)
         wait(sums[0][1])
         sy[yi] = sum4(sz)
         start(sums[1][0])
-        do_f(4)
-        do_b1(5)
+        do_f(5)
+        do_cols(2)
         wait(sums[1][1])
         sx[xi] = sum4(sy)
         start(sums[2][0])
-        do_b2(5)
-        do_f(5)
-        do_cols(1)
+        do_assemble(1)
 
         for q in PAIR:
             rows = h_ref[:, pl.ds(pl.multiple_of(core * TS + q * TB, TB), TB)].astype(F32)
@@ -696,8 +782,6 @@
             dz[core, 3, q] = inv * (gu - unit * jnp.mean(gu * unit, axis=0, keepdims=True))
         half_copy = remote(dz.at[core, 3], uf.at[7], hs, hr, {"tp": other})
         half_copy.start()
-        do_assemble(0)
-        do_assemble(1)
         wait(sums[2][1])
         sum_out[...] = sum4(sx)
         sum_out[ROW1, span(0, TB)] = sum_out[ROW1, span(0, TB)] / aux[1, ROW1, :]
@@ -706,10 +790,12 @@
             for q in PAIR:
                 gb[half, q] = jnp.where(core == half, dz[core, 3, q], uf[7, q]).astype(BF16)
                 out_dh(half, q).start()
+        do_assemble(2)
         wait([out_dh(half, q) for half in PAIR for q in PAIR])
+        wait([out_de(b, x) for b in BATCHES for x in QUAD])
 
         sent(gmine + gonward + [gpcopy(r, q) for r in HOPS for q in PAIR] + [dcopy(r) for r in QUAD])
-        sent([col(b, dy, dx) for b in PAIR for dy, dx in FAR])
+        sent([col(b, dy, dx) for b in BATCHES for dy, dx in FAR])
     pl.run_scoped(
         backward, V((2, GX, 2, D, TB), F32), V((2 * NP, 16, ROWS, LANE), F32), V((2, NS, V2, TS), F32), V((2, D, EC), BF16)
     )
@@ -718,7 +804,7 @@
         sent(stat_copies(r))
 
 
-def call(h_t, ge_t, w, ints, et):
+def call(*args):
     links = [DMA((2, 2, 2))] * 8
     return pl.pallas_call(
         kernel,
@@ -726,8 +812,8 @@
             SDS((OWN, VL), F32), SDS((D, TOK), BF16), SDS(SUMS, F32),
             SDS((NS, VB, TS), F32), SDS(TOKENS, F32), SDS(TOKENS, F32),
         ),
-        in_specs=[VMEM, ANY, VMEM, VMEM, ANY],
-        out_specs=(VMEM, ANY, VMEM) + (ANY,) * 3,
+        in_specs=[VMEM, ANY] + [VMEM] * 4 + [ANY],
+        out_specs=(ANY, ANY, VMEM) + (ANY,) * 3,
         scratch_shapes=[
             V(TOKENS, F32),
             *[V(TOKENS, BF16)] * 2,
@@ -736,32 +822,31 @@
             V((NS, GX, SUB, TB), F32), V((1, TB), F32),
             *[V((GX, SUB, LANE), F32)] * 2,
             V((NS, 2, TS), F32), V((NS, 2, TS), I32), V((2, SUB, TB), F32),
+            V((D, LANE), F32),
+            V((OWN, VL), F32),
             V((2, 2, 2, 2, ROWS, LANE), F32),
             V((2, 2, 2, GX, ROWS, LANE), F32),
             V((2, 2, 2, HROWS, LANE), F32),
             V((2, 2, 2, ROWS, LANE), F32),
-            *[V((2, 16, 56, LANE), F32)] * 2,
+            *[V((3, 16, 40, LANE), F32)] * 2,
             V((2, *SUMS), F32), *[V((GX, *SUMS), F32)] * 3,
-            DMA((3,)), DMA((2,)), DMA((2, 2)), *[DMA((2,))] * 2, DMA((2, 2)), *[DMA((NS, 2))] * 2,
+            DMA((3, GX)), DMA((2 * NP,)), DMA((2,)), DMA((2, 2)), *[DMA((2,))] * 2, DMA((2, 2)), *[DMA((NS, 2))] * 2,
             DMA((NS,)), *[DMA((GX, 2))] * 3, *[DMA((GX,))] * 2, *[DMA((NS, GX))] * 2, *[DMA((2, GX))] * 2,
             DMA((NS,)), *[DMA((GX, 2))] * 3, *links,
-            *[DMA((2, 16))] * 2, *[DMA((GX,))] * 2, *[DMA((2, 2))] * 2, *[DMA((2,))] * 2, *[DMA(())] * 4, *[DMA((3, GX))] * 2,
+            *[DMA((3, 16))] * 2, *[DMA((GX,))] * 2, *[DMA((2, 2))] * 2, *[DMA((2,))] * 2, *[DMA(())] * 4, *[DMA((3, GX))] * 2,
         ],
         compiler_params=pltpu.CompilerParams(vmem_limit_bytes=67043328, collective_id=0, has_side_effects=True),
-    )(h_t, ge_t, w, ints, et)
+    )(*args)
 
 
 def solution(mesh):
-    mesh4 = Mesh(mesh.devices.reshape(2, 4, 4, 4), ("tp", "z", "y", "x"))
+    mesh4 = Mesh(mesh.devices.reshape(2, GX, GX, GX), ("tp", "z", "y", "x"))
 
     def local_step(hidden, norm_w, embed, targets, loss_mask, token_ids, grad_embed):
-        base = lax.axis_index("tp") * VL
         h_t = hidden.reshape(TOK, D).T
         ge_t = grad_embed.reshape(TOK, D).T
-        own = [a.reshape(2, 2, 1, TB) for a in (targets - base, token_ids - base, loss_mask)]
-        ints = jnp.concatenate(own + own[:1] * 5, axis=2)
-        de, dh, sums, *_ = call(h_t, ge_t, norm_w.reshape(D, 1), ints, embed.T)
-        return sums[1, 0], dh.T.reshape(1, TOK, D), sums[0, :D], de.T
+        de, dh, sums, *_ = call(h_t, ge_t, norm_w.reshape(D, 1), targets, loss_mask, token_ids, embed.T)
+        return sums[1, 0], dh.T.reshape(hidden.shape), sums[0, :D], de.T
 
     dp = ("z", "y", "x")
     return jax.shard_map(

time: 244 us -> 232 us (0.951); the launches traced: 240 us -> 232 us
  Pallas kernels: 230 us -> 224 us
    pallas_call x1, Pallas kernels: 230 us -> 224 us  [call(): pl.pallas_call(kernel, out_shape=(SDS((OWN, VL), F32), SDS((D, TOK), BF16...]
where the time goes in v5:
time: 232 us
  Pallas kernels  224 us (97%)
  local copies, waits for them, and re-layouts  7.59 us (3%)
    pallas_call x1, Pallas kernels, call(): pl.pallas_call(kernel, out_shape=(SDS((OWN, VL), F32), SDS((D, TOK), BF16...  224 us

profile of v5, /device:TPU:1, one launch (start us, length us, event | category | flops | bytes accessed | tf_op | source)
XLA Modules:
  0.0 231.8 jit_solution(17395888606501518934)
XLA Ops:
  0.6 1.5 reshape.24.w_ref
  2.1 223.6 %shard_map.102 = (f32[9,24576]{1,0:T(8,128)}, bf16[576,1024]{1,0:T(8,128)(2,1)}, f32[2,640]{1,0:T(2,128)}, f32[8,6144,512]{2,1,0:T(8,128)}, f32[8,2,576,256]{3,2,1,0:T(8,128)}, /*index=5*/f32[8,2,576,256]{3,2,1,0:T(8,128)}) custom-call(bf16[576,1024]{1,0:T(8,128)(2,1)} %bitcast.14, bf16[576,1024]{1,0:T(8,128)(2,1)} %bitcast.15, ...), custom_call_target="tpu_custom_call" | custom-call | tf_op jit(solution)/shard_map/pallas_call | solution.py:809
  225.7 0.0 copy-start
  225.7 1.3 slice.6
  227.0 1.3 slice_reduce_fusion
  228.3 2.4 %copy.14 = bf16[1,1024,576]{1,2,0:T(8,128)(2,1)} copy(bf16[1,1024,576]{1,2,0:T(8,128)(2,1)} %bitcast.16) | data formatting | bytes 2359296
  230.7 0.0 copy-done
  230.7 1.1 copy.15
Async XLA Ops:
  225.7 5.0 %copy-start = (f32[9,24576]{1,0:T(8,128)S(1)}, f32[9,24576]{1,0:T(8,128)}, u32[]{:S(2)}) copy-start(f32[9,24576]{1,0:T(8,128)} %get-tuple-element.9) | copy-start | bytes 2654212

commit v6 on v5

--- a/solution.py
+++ b/solution.py
@@ -197,10 +197,6 @@
                 rows = h_ref[:, pl.ds(half * TS + q * TB, TB)].astype(F32)
                 inv = lax.rsqrt(jnp.mean(rows * rows, axis=0, keepdims=True) + RMS_EPS)
                 uf[half, q] = rows * inv
-        wait([own_ge(half, q) for half in PAIR for q in PAIR])
-        for q in PAIR:
-            gst[q] = gb[core, q].astype(F32)
-        start([keep_ge(q) for q in PAIR])
 
         def ebody(i, _):
             etcopy(i).wait()
@@ -209,11 +205,14 @@
             return 0
 
         lax.fori_loop(0, 2 * NP, ebody, 0)
-        wait([keep_ge(q) for q in PAIR])
         pl.semaphore_wait(barrier, len(peers))
         start(own[:2])
         start([icopy(d) for d in HOPS])
         start(own[2:])
+        wait([own_ge(half, q) for half in PAIR for q in PAIR])
+        for q in PAIR:
+            gst[q] = gb[core, q].astype(F32)
+        start([keep_ge(q) for q in PAIR])
         iota = lax.broadcasted_iota(I32, (SUB, TB), 0)
 
         def ocopy(ts, q, slot):
@@ -234,6 +233,7 @@
                     pcopy(r, q).start()
                 arrive([icopy(d) for d in HOPS])
                 start(stat_copies(0))
+                wait([keep_ge(q) for q in PAIR])
                 start(gmine[:2])
 
             @pl.when(s == 6)

time: 232 us -> 230 us (level)
  Pallas kernels: 224 us -> 221 us
where the time goes in v6:
time: 230 us
  Pallas kernels  221 us (96%)
  local copies, waits for them, and re-layouts  7.59 us (3%)
    pallas_call x1, Pallas kernels, call(): pl.pallas_call(kernel, out_shape=(SDS((OWN, VL), F32), SDS((D, TOK), BF16...  221 us

profile of v6, /device:TPU:1, one launch (start us, length us, event | category | flops | bytes accessed | tf_op | source)
XLA Modules:
  0.0 229.5 jit_solution(16772820210629337792)
XLA Ops:
  0.6 1.5 reshape.24.w_ref
  2.1 221.3 %shard_map.102 = (f32[9,24576]{1,0:T(8,128)}, bf16[576,1024]{1,0:T(8,128)(2,1)}, f32[2,640]{1,0:T(2,128)}, f32[8,6144,512]{2,1,0:T(8,128)}, f32[8,2,576,256]{3,2,1,0:T(8,128)}, /*index=5*/f32[8,2,576,256]{3,2,1,0:T(8,128)}) custom-call(bf16[576,1024]{1,0:T(8,128)(2,1)} %bitcast.14, bf16[576,1024]{1,0:T(8,128)(2,1)} %bitcast.15, ...), custom_call_target="tpu_custom_call" | custom-call | tf_op jit(solution)/shard_map/pallas_call | solution.py:809
  223.4 0.0 copy-start
  223.4 1.3 slice.6
  224.7 1.3 slice_reduce_fusion
  226.0 2.4 %copy.14 = bf16[1,1024,576]{1,2,0:T(8,128)(2,1)} copy(bf16[1,1024,576]{1,2,0:T(8,128)(2,1)} %bitcast.16) | data formatting | bytes 2359296
  228.4 0.0 copy-done
  228.4 1.1 copy.15
Async XLA Ops:
  223.4 5.0 %copy-start = (f32[9,24576]{1,0:T(8,128)S(1)}, f32[9,24576]{1,0:T(8,128)}, u32[]{:S(2)}) copy-start(f32[9,24576]{1,0:T(8,128)} %get-tuple-element.9) | copy-start | bytes 2654212
